TPU v7x, 256 devices: a whole 4x4x8 slice. The times are simulated.
256 devices in a mesh: expert: 64 (over z, x, core), shard: 4 (over y).
Axes of the slice: x: 4, y: 4, z: 8, core: 2. Of those that a mesh axis runs over, the one named last changes fastest.
Arguments:
- master_down: float32 [128, 768, 2048], P('expert', None, 'shard'), may hold values from -0.3125 to 0.3125
- router_weight: float32 [2048, 128], P('shard', 'expert'), may hold values from -0.125 to 0.125
- router_gain: float32 [2048], P('shard'), may hold values from 0.25 to 1.75
Outputs:
- final_down: bfloat16 [128, 768, 2048], P('expert')
- scale_down: float32 [128, 768], P('expert')
- serve_router: bfloat16 [2048, 128], replicated
All inputs are finite; a program needn't handle non-finite values.
Results may differ from a plain program's by a relative error of at most 0.001.
Values may be sent and summed in bfloat16 or wider, within the bound.
A program may use at most 64 MiB of HBM per device.

v0:
```python
import jax
import jax.numpy as jnp
from jax import lax
from jax.sharding import Mesh
from jax.sharding import PartitionSpec as P

EXPERT = ("expert_0", "expert_1", "expert_2")


def sent_to_all(shard, axis):
    length = lax.axis_size(axis)
    return lax.all_to_all(
        jnp.broadcast_to(shard[None], (length, *shard.shape)), axis, 0, 0, tiled=True
    )


def taken_together(shard, axis):
    return sent_to_all(shard, axis).sum(axis=0)


def joined_along(blocks, dim):
    blocks = jnp.moveaxis(blocks, 0, dim)
    lengths = blocks.shape
    return blocks.reshape(*lengths[:dim], lengths[dim] * lengths[dim + 1], *lengths[dim + 2 :])


def gather_in_order(shard, axes, turns):
    blocks = shard
    for k in turns:
        blocks = lax.all_gather(blocks, axes[k])
    done = turns[::-1]
    back = [done.index(k) for k in range(len(axes))]
    blocks = blocks.transpose(*back, *range(len(axes), blocks.ndim))
    return blocks.reshape(-1, *shard.shape)


def gathered_by_axis(shard, axes, turns, dim):
    return joined_along(gather_in_order(shard, axes, turns), dim)


def body(master_down, router_weight, router_gain):
    total_down = taken_together(jnp.sum(master_down * master_down, axis=2), "shard")
    scale_down = jnp.sqrt(total_down)
    narrow_down = (master_down / jnp.expand_dims(scale_down, 2)).astype(jnp.bfloat16)
    final_down = lax.all_gather(narrow_down, "shard", axis=2, tiled=True)
    part_router = (router_weight * router_gain[:, None]).astype(jnp.bfloat16)
    row_router = lax.all_gather(part_router, "shard", axis=0, tiled=True)
    serve_router = gathered_by_axis(row_router, EXPERT, (1, 0, 2), 1)
    return (final_down, scale_down, serve_router)


def solution(mesh):
    finer = Mesh(
        mesh.devices.reshape(8, 4, 2, mesh.shape["shard"]),
        ("expert_0", "expert_1", "expert_2", "shard"),
    )
    in_specs = (P(EXPERT, None, "shard"), P("shard", EXPERT), P("shard"))
    out_specs = (P(EXPERT, None, None), P(EXPERT, None), P())
    return jax.shard_map(body, mesh=finer, in_specs=in_specs, out_specs=out_specs, check_vma=False)
```

profile of v0, /device:TPU:2, one launch (start us, length us, event | category | flops | bytes accessed | tf_op | source)
XLA Modules:
  0.0 103.5 jit_solution(8740039079372354039)
XLA Ops:
  7.2 0.0 copy-start
  7.2 0.0 all-gather.5.cloned.1.call-start
  7.2 2.3 %multiply_reduce_fusion = f32[2,768]{1,0:T(2,128)S(1)} fusion(f32[2,768,512]{2,1,0:T(8,128)} %param.3), kind=kLoop, calls=%fused_computation.1 | loop fusion | flops 1571328 | bytes 3151872 | tf_op jit(solution)/shard_map/reduce_sum | solution.py:42
  9.6 9.7 %all_to_all.5 = f32[4,2,768]{2,1,0:T(2,128)S(1)} all-to-all(f32[4,2,768]{2,1,0:T(2,128)S(1)} %broadcast_in_dim.2), channel_id=1, replica_groups=mesh['expert_0'=8,'expert_1'=4,'expert_2'=2,'shard'=4] {'shard'}, dimensions={0} | all-to-all | bytes 49152 | tf_op jit(solution)/shard_map/all_to_all | solution.py:12
  19.3 0.0 copy-done
  19.3 0.0 copy-start.1
  19.3 0.0 copy-start.2
  19.3 0.0 copy-start.3
  19.3 1.4 %divide_convert_fusion = bf16[2,768,512]{2,1,0:T(8,128)(2,1)} fusion(f32[2,768,512]{2,1,0:T(8,128)S(1)} %copy-done, f32[2,768]{1,0:T(2,128)S(1)} %sqrt.7), kind=kLoop, calls=%fused_computation | loop fusion | flops 1572864 | bytes 4724736 | tf_op jit(solution)/shard_map/convert_element_type | solution.py:44
  20.8 0.0 all-gather.5.cloned.1.call-update
  20.8 0.0 copy-done.1
  20.8 0.0 copy-done.2
  20.8 0.0 copy-done.3
  20.8 10.4 %all_gather.25 = bf16[2048,2]{0,1:T(2,128)(2,1)S(1)} all-gather(bf16[512,2]{0,1:T(2,128)(2,1)S(1)} %multiply_convert_fusion), channel_id=1, replica_groups=mesh['expert_0'=8,'expert_1'=4,'expert_2'=2,'shard'=4] {'shard'}, dimensions={0}, use_global_device_ids=true | all-gather | bytes 10240 | tf_op jit(solution)/shard_map/all_gather | solution.py:47
  31.3 12.0 %all-gather = bf16[8192,2]{0,1:T(2,128)(2,1)S(1)} all-gather(bf16[2048,2]{0,1:T(2,128)(2,1)S(1)} %all_gather.25), channel_id=2, replica_groups=mesh['expert_0'=8,'expert_1'=4,'expert_2'=2,'shard'=4] {'expert_1'}, dimensions={0}, use_global_device_ids=true | all-gather | bytes 40960 | tf_op jit(solution)/shard_map/all_gather | solution.py:30
  43.2 28.5 %all-gather.1 = bf16[32,2048,2]{1,2,0:T(2,128)(2,1)S(1)} all-gather(bf16[4,2048,2]{1,2,0:T(2,128)(2,1)S(1)} %bitcast.15), channel_id=3, replica_groups=mesh['expert_0'=8,'expert_1'=4,'expert_2'=2,'shard'=4] {'expert_0'}, dimensions={0}, use_global_device_ids=true | all-gather | bytes 294912 | tf_op jit(solution)/shard_map/all_gather | solution.py:30
  71.7 0.1 copy.20
  71.8 2.2 %all-gather.2 = bf16[16,4,2048,2]{2,1,3,0:T(4,128)(2,1)S(1)} all-gather(bf16[8,4,2048,2]{2,1,3,0:T(4,128)(2,1)S(1)} %copy.20), channel_id=4, replica_groups=mesh['expert_0'=8,'expert_1'=4,'expert_2'=2,'shard'=4] {'expert_2'}, dimensions={0}, use_global_device_ids=true | all-gather | bytes 786432 | tf_op jit(solution)/shard_map/all_gather | solution.py:30
  74.0 0.3 copy.26
  74.3 0.5 copy.22
  74.9 0.2 reshape.18
  75.1 1.0 copy.23
  76.1 14.0 %all-gather.5.cloned.1.call-done = bf16[2,768,2048]{2,1,0:T(8,128)(2,1)} async-done(((bf16[2,768,512]{2,1,0:T(8,128)(2,1)}), bf16[2,768,2048]{2,1,0:T(8,128)(2,1)}) %all-gather.5.cloned.1.call-update) | async-done | bytes 6291472 | tf_op jit(solution)/shard_map/all_gather | solution.py:45
  90.1 6.6 %copy.28 = bf16[2,768,2048]{2,1,0:T(8,128)(2,1)} copy(bf16[2,768,2048]{2,1,0:T(8,128)(2,1)} %all-gather.5.cloned.1.call-done) | data formatting | bytes 12582912
  (4 shorter events, 0.0 us)
Async XLA Ops:
  7.2 12.1 %copy-start = (f32[2,768,512]{2,1,0:T(8,128)S(1)}, f32[2,768,512]{2,1,0:T(8,128)}, u32[]{:S(2)}) copy-start(f32[2,768,512]{2,1,0:T(8,128)} %param.3) | copy-start | bytes 9437188
  7.2 82.9 %all-gather.5.cloned.1.call-start = ((), (), s32[]{:S(2)}) async-start(), calls=%async_computation.1 | async-start | bytes 7864320 | tf_op jit(solution)/shard_map/all_gather | solution.py:45
  19.3 1.5 %copy-start.1 = (f32[2,768]{1,0:T(2,128)}, f32[2,768]{1,0:T(2,128)S(1)}, u32[]{:S(2)}) copy-start(f32[2,768]{1,0:T(2,128)S(1)} %sqrt.7) | copy-start | bytes 18436
  19.3 1.5 %copy-start.2 = (f32[512,2]{0,1:T(2,128)S(1)}, f32[512,2]{0,1:T(2,128)}, u32[]{:S(2)}) copy-start(f32[512,2]{0,1:T(2,128)} %param.4) | copy-start | bytes 12292
  19.3 1.5 %copy-start.3 = (f32[512]{0:T(512)S(1)}, f32[512]{0:T(512)}, u32[]{:S(2)}) copy-start(f32[512]{0:T(512)} %param.5) | copy-start | bytes 6148
Sparse Core Ops, SparseCore 0:
  20.9 69.1 all-gather.4
where the time goes:
time: 104 us
  blocking collectives  62.7 us (60%)
  between operations  14.1 us (14%)
  waiting for transfers between devices  14 us (13%)
  local copies, waits for them, and re-layouts  8.83 us (8%)
  other arithmetic  3.79 us (4%)
    all_gather x3, blocking collectives, gather_in_order(): blocks = lax.all_gather(blocks, axes[k])  42.6 us
    all_gather x1, waiting for transfers between devices, body(): final_down = lax.all_gather(narrow_down, 'shard', axis=2, tiled=True)  14 us
    all_gather x1, blocking collectives, body(): row_router = lax.all_gather(part_router, 'shard', axis=0, tiled=True)  10.4 us
    all_to_all x1, blocking collectives, sent_to_all(): lax.all_to_all(jnp.broadcast_to(shard[None], (length, *shard.shape)), axi...  9.67 us
    unnamed x10, local copies, waits for them, and re-layouts  7.64 us
    reduce_sum x1, other arithmetic, body(): jnp.sum(master_down * master_down, axis=2)  2.33 us
  transfers between devices with their start and end apart: 1, of which 1 were waited for; matrix products, arithmetic and copies ran while one was open for 2% of the time, Pallas kernels for 0%

commit v1 on v0

v1 whole, which is shorter than its diff:
```python
import functools

import jax
import jax.numpy as jnp
from jax import lax
from jax.experimental import pallas as pl
from jax.experimental.pallas import tpu as pltpu
from jax.sharding import Mesh
from jax.sharding import PartitionSpec as P

MESH = pl.DeviceIdType.MESH
EXPERT = ("z", "x", "core")
BF16, F32 = jnp.bfloat16, jnp.float32

BLOCK = 128
GROUPS = BLOCK // 8
PARTS = ((0, 2), (2, 7), (7, 12))
CHUNKS = ((0, 1), (1, 2), (2, 4), (4, 6), (6, 8), (8, 10), (10, 12))
HALF = 4


def part_of(block):
    for p, (lo, hi) in enumerate(PARTS):
        if lo <= block < hi:
            return p, (block - lo) * GROUPS


def pick(first):
    lane = lax.broadcasted_iota(jnp.int32, (GROUPS, 8, 128), 2)
    group = lax.broadcasted_iota(jnp.int32, (GROUPS, 8, 128), 0)
    return lane == group + first


def column(packed, block):
    p, first = part_of(block)
    spread = jnp.where(pick(first), packed[p][None], 0.0)
    return jnp.sum(spread, axis=2, keepdims=True).reshape(BLOCK, 1)


def gather_kernel(
    master, router, gain,
    gathered, scale_out, router_out,
    rows, sums, wide, weight, gains, pieces, tall,
    load_sem, small_sem, sum_send, sum_recv, up_send, up_recv, down_send, down_recv,
    fwd_up_send, fwd_up_recv, fwd_down_send, fwd_down_recv,
    ry_send, ry_recv, rc_send, rc_recv, rx_send, rx_recv, zu_send, zu_recv, zd_send, zd_recv,
):
    z, x, core, y = (lax.axis_index(a) for a in ("z", "x", "core", "shard"))
    nz, nx, ny = 8, 4, 4
    mine = z * (nx * 2) + x * 2 + core

    def at_y(step):
        return (z, x, core, lax.rem(y + step, ny))

    def at_x(step):
        return (z, lax.rem(x + step, nx), core, y)

    def at_z(step):
        return (lax.rem(z + step, nz), x, core, y)

    partner = (z, x, 1 - core, y)

    loads = []
    for p, (lo, hi) in enumerate(PARTS):
        view = pl.ds(lo * BLOCK, (hi - lo) * BLOCK)
        loads.append(pltpu.make_async_copy(master.at[view], rows.at[view], load_sem.at[p]))
        loads[-1].start()
    small = [
        pltpu.make_async_copy(router, weight, small_sem.at[0]),
        pltpu.make_async_copy(gain, gains, small_sem.at[1]),
    ]
    for copy in small:
        copy.start()

    barrier = pltpu.get_barrier_semaphore()
    peers = [at_y(1), at_y(2), at_y(3), at_x(1), at_x(2), at_x(3), partner, at_z(1), at_z(nz - 1)]
    for peer in peers:
        pl.semaphore_signal(barrier, inc=1, device_id=peer, device_id_type=MESH)

    def remote(src, dst, send, recv, peer):
        copy = pltpu.make_async_remote_copy(
            src_ref=src, dst_ref=dst, send_sem=send, recv_sem=recv, device_id=peer, device_id_type=MESH
        )
        return copy

    def partial_sums(p):
        lo, hi = PARTS[p]
        loads[p].wait()
        packed = jnp.zeros((8, 128), F32)
        for block in range(lo, hi):
            values = rows[pl.ds(block * BLOCK, BLOCK), :]
            total = jnp.sum(values * values, axis=1, keepdims=True).reshape(GROUPS, 8, 1)
            packed = packed + jnp.sum(jnp.where(pick((block - lo) * GROUPS), total, 0.0), axis=0)
        sums[y, p] = packed

    def send_sums(first, count, slot):
        out = []
        for d in (1, 3, 2):
            view = sums.at[y, pl.ds(first, count)]
            out.append(remote(view, view, sum_send.at[slot, d - 1], sum_recv.at[slot, d - 1], at_y(d)))
            out[-1].start()
        return out

    partial_sums(0)
    for copy in small:
        copy.wait()
    pieces[y, mine] = (weight[...] * gains[...]).astype(BF16)
    pl.semaphore_wait(barrier, len(peers))
    sum_copies = [send_sums(0, 1, 0)]
    partial_sums(1)
    partial_sums(2)
    sum_copies.append(send_sums(1, 2, 1))

    view = pieces.at[y, mine]
    ry = [remote(view, view, ry_send.at[d - 1], ry_recv.at[d - 1], at_y(d)) for d in (1, 2, 3)]
    for copy in ry:
        copy.start()

    inverse = {}

    def finish_sums(slot, parts):
        for copy in sum_copies[slot]:
            copy.wait_recv()
        for p in parts:
            scale = jnp.sqrt((sums[0, p] + sums[1, p]) + (sums[2, p] + sums[3, p]))
            wide[p] = scale
            inverse[p] = 1.0 / scale

    def chunk_view(owner, c):
        lo, hi = CHUNKS[c]
        return gathered.at[owner, pl.ds(lo * BLOCK, (hi - lo) * BLOCK)]

    bulk = []
    finish_sums(0, (0,))
    for c, (lo, hi) in enumerate(CHUNKS):
        if lo == PARTS[1][0]:
            finish_sums(1, (1, 2))
        for block in range(lo, hi):
            view = pl.ds(block * BLOCK, BLOCK)
            gathered[y, view, :] = (rows[view, :] * column(inverse, block)).astype(BF16)
        view = chunk_view(y, c)
        bulk.append(remote(view, view, up_send.at[c], up_recv.at[c], at_y(1)))
        bulk.append(remote(view, view, down_send.at[c], down_recv.at[c], at_y(3)))
        bulk[-2].start()
        bulk[-1].start()

    for copy in ry:
        copy.wait_recv()
    view = pieces.at[:, mine]
    rc = remote(view, view, rc_send, rc_recv, partner)
    rc.start()
    scales = [wide[p] for p in range(len(PARTS))]
    for block in range(12):
        same = lax.broadcasted_iota(jnp.int32, (BLOCK, 128), 0) == lax.broadcasted_iota(jnp.int32, (BLOCK, 128), 1)
        line = jnp.sum(jnp.where(same, column(scales, block), 0.0), axis=0, keepdims=True)
        scale_out[block // 6 : block // 6 + 1, (block % 6) * 128 : (block % 6 + 1) * 128] = line
    rc.wait_recv()
    view = pieces.at[:, pl.ds(z * 8 + x * 2, 2)]
    rx = [remote(view, view, rx_send.at[d - 1], rx_recv.at[d - 1], at_x(d)) for d in (1, 2, 3)]
    for copy in rx:
        copy.start()
    for copy in rx:
        copy.wait_recv()
    zu, zd = [], []
    for k in range(4):
        if k:
            zu[-1].wait_recv()
        view = pieces.at[:, pl.ds(lax.rem(z + nz - k, nz) * 8, 8)]
        zu.append(remote(view, view, zu_send.at[k], zu_recv.at[k], at_z(1)))
        zu[-1].start()
        if k < 3:
            if k:
                zd[-1].wait_recv()
            view = pieces.at[:, pl.ds(lax.rem(z + k, nz) * 8, 8)]
            zd.append(remote(view, view, zd_send.at[k], zd_recv.at[k], at_z(nz - 1)))
            zd[-1].start()

    forwards = []
    for k in range(HALF):
        bulk[2 * k].wait_recv()
        view = chunk_view(lax.rem(y + 3, ny), k)
        forwards.append(remote(view, view, fwd_up_send.at[k], fwd_up_recv.at[k], at_y(1)))
        forwards[-1].start()
        if k + HALF < len(CHUNKS):
            c = k + HALF
            bulk[2 * c + 1].wait_recv()
            view = chunk_view(lax.rem(y + 1, ny), c)
            forwards.append(remote(view, view, fwd_down_send.at[k], fwd_down_recv.at[k], at_y(3)))
            forwards[-1].start()

    zu[-1].wait_recv()
    zd[-1].wait_recv()

    def lay(step, _):
        for s in range(ny):
            four = [pieces[s, step * 4 + i].astype(F32) for i in range(4)]
            tall[pl.ds(pl.multiple_of(step * 8, 8), 8), s * 512 : (s + 1) * 512] = jnp.concatenate(four, axis=0)
        return 0

    lax.fori_loop(0, 16, lay, 0)
    for i in range(16):
        router_out[i * 128 : (i + 1) * 128, :] = tall[:, i * 128 : (i + 1) * 128].T.astype(BF16)

    for c in range(len(CHUNKS)):
        if c >= HALF:
            bulk[2 * c].wait_recv()
        else:
            bulk[2 * c + 1].wait_recv()
    for copy in forwards:
        copy.wait_recv()
    for copy in bulk + forwards + ry + [rc] + rx + zu + zd:
        copy.wait_send()
    for copies in sum_copies:
        for copy in copies:
            copy.wait_send()


def write_kernel(gathered, scale, router, down_out, scale_out, router_out, sems):
    copies = [
        pltpu.make_async_copy(gathered.at[s], down_out.at[:, pl.ds(s * 512, 512)], sems.at[s]) for s in range(4)
    ]
    copies.append(pltpu.make_async_copy(scale, scale_out, sems.at[4]))
    copies.append(pltpu.make_async_copy(router, router_out, sems.at[5]))
    for copy in copies:
        copy.start()
    for copy in copies:
        copy.wait()


def body(master_down, router_weight, router_gain):
    dma = pltpu.SemaphoreType.DMA
    n = len(CHUNKS)
    hbm = pl.BlockSpec(memory_space=pltpu.HBM)
    vmem = pl.BlockSpec(memory_space=pltpu.VMEM)
    gathered, scale, router = pl.pallas_call(
        gather_kernel,
        name="gather",
        out_shape=(
            pltpu.VMEM((4, 1536, 512), BF16),
            pltpu.VMEM((2, 768), F32),
            pltpu.VMEM((2048, 128), BF16),
        ),
        in_specs=[hbm] * 3,
        out_specs=[vmem] * 3,
        scratch_shapes=[
            pltpu.VMEM((1536, 512), F32),
            pltpu.VMEM((4, 3, 8, 128), F32),
            pltpu.VMEM((3, 8, 128), F32),
            pltpu.VMEM((2, 512), F32),
            pltpu.VMEM((1, 512), F32),
            pltpu.VMEM((4, 64, 2, 512), BF16),
            pltpu.VMEM((128, 2048), F32),
            dma((3,)), dma((2,)), dma((2, 3)), dma((2, 3)), dma((n,)), dma((n,)), dma((n,)), dma((n,)),
            dma((HALF,)), dma((HALF,)), dma((HALF,)), dma((HALF,)),
            dma((3,)), dma((3,)), dma(()), dma(()), dma((3,)), dma((3,)), dma((4,)), dma((4,)), dma((3,)), dma((3,)),
        ],
        compiler_params=pltpu.CompilerParams(collective_id=0, has_side_effects=True, vmem_limit_bytes=32 << 20),
    )(master_down.reshape(1536, 512), router_weight.T, router_gain.reshape(1, 512))
    down, scale, router = pl.pallas_call(
        write_kernel,
        name="write",
        out_shape=(
            jax.ShapeDtypeStruct((1536, 2048), BF16),
            jax.ShapeDtypeStruct((2, 768), F32),
            jax.ShapeDtypeStruct((2048, 128), BF16),
        ),
        in_specs=[vmem] * 3,
        out_specs=[hbm] * 3,
        scratch_shapes=[dma((6,))],
    )(gathered, scale, router)
    return down.reshape(2, 768, 2048), scale, router


def solution(mesh):
    finer = Mesh(mesh.devices.reshape(8, 4, 2, mesh.shape["shard"]), (*EXPERT, "shard"))
    in_specs = (P(EXPERT, None, "shard"), P("shard", EXPERT), P("shard"))
    out_specs = (P(EXPERT, None, None), P(EXPERT, None), P())
    return jax.shard_map(body, mesh=finer, in_specs=in_specs, out_specs=out_specs, check_vma=False)
```

time: 104 us -> 77 us (0.74)
  Pallas kernels: 0 us -> 68.8 us
  blocking collectives: 62.7 us -> 0 us
  waiting for transfers between devices: 14 us -> 0 us
  between operations: 14.1 us -> 0.66 us
  other arithmetic: 3.79 us -> 0 us
  local copies, waits for them, and re-layouts: 8.83 us -> 7.3 us
    pallas_call x0 -> x2, Pallas kernels: none -> 68.8 us  [the longest x1 63.1 us: body(): pl.pallas_call(gather_kernel, name='gather', out_shape=(pltpu.VMEM((4, 15...]
    all_gather x4 -> x0, blocking collectives: 53.1 us -> none  [the longest x3 42.6 us: gather_in_order(): blocks = lax.all_gather(blocks, axes[k])]
    all_gather x1 -> x0, waiting for transfers between devices: 14 us -> none  [body(): final_down = lax.all_gather(narrow_down, 'shard', axis=2, tiled=True)]
    all_to_all x1 -> x0, blocking collectives: 9.67 us -> none  [sent_to_all(): lax.all_to_all(jnp.broadcast_to(shard[None], (length, *shard.shape)), axi...]
    reduce_sum x2 -> x0, other arithmetic: 2.35 us -> none  [the longest x1 2.33 us: body(): jnp.sum(master_down * master_down, axis=2)]
    convert_element_type x2 -> x0, other arithmetic: 1.44 us -> none  [the longest x1 1.43 us: body(): (master_down / jnp.expand_dims(scale_down, 2)).astype(jnp.bfloat16)]
    unnamed x10 -> x12, local copies, waits for them, and re-layouts: 7.64 us -> 7.3 us
  transfers between devices with their start and end apart: 1 -> 0, of which waited for: 1 -> 0; matrix products, arithmetic and copies ran while one was open for 2% -> 0% of each run, Pallas kernels for 0% -> 0%
where the time goes in v1:
time: 77 us; the launch traced here: 76.8 us
  Pallas kernels  68.8 us (89%)
  local copies, waits for them, and re-layouts  7.3 us (9%)
    pallas_call x1, Pallas kernels, body(): pl.pallas_call(gather_kernel, name='gather', out_shape=(pltpu.VMEM((4, 15...  63.1 us
    unnamed x12, local copies, waits for them, and re-layouts  7.3 us
    pallas_call x1, Pallas kernels, body(): pl.pallas_call(write_kernel, name='write', out_shape=(jax.ShapeDtypeStruc...  5.75 us

profile of v1, /device:TPU:2, one launch (start us, length us, event | category | flops | bytes accessed | tf_op | source)
XLA Modules:
  0.0 76.8 jit_solution(16635766782013955507)
XLA Ops:
  0.6 0.0 copy-start.1
  0.6 1.9 %copy-done.1 = f32[2,768,512]{2,1,0:T(8,128)S(1)} copy-done((f32[2,768,512]{2,1,0:T(8,128)S(1)}, f32[2,768,512]{2,1,0:T(8,128)}, u32[]{:S(2)}) %copy-start.1) | copy-done | bytes 3145752
  2.5 0.0 copy-start.4
  2.5 0.7 copy-done.4
  3.2 0.0 copy-start.5
  3.2 0.7 copy-done.5
  3.9 63.1 %gather.1 = (bf16[4,1536,512]{2,1,0:T(8,128)(2,1)S(1)}, f32[2,768]{1,0:T(2,128)S(1)}, bf16[2048,128]{1,0:T(8,128)(2,1)S(1)}) custom-call(f32[1536,512]{1,0:T(8,128)S(1)} %bitcast.4, f32[2,512]{1,0:T(2,128)S(1)} %bitcast.5, f32[1,512]{1,0:T(1,128)S(1)} %bitcast.6), custom_call_target="tpu_custom_call" | custom-call | tf_op jit(solution)/shard_map/gather/pallas_call | solution.py:235
  67.0 0.0 copy-start
  67.0 2.6 %copy-done = bf16[4,1536,512]{2,1,0:T(8,128)(2,1)} copy-done((bf16[4,1536,512]{2,1,0:T(8,128)(2,1)}, bf16[4,1536,512]{2,1,0:T(8,128)(2,1)S(1)}, u32[]{:S(2)}) %copy-start) | copy-done | bytes 6291480
  69.6 0.0 copy-start.2
  69.6 0.8 %copy-done.2 = bf16[2048,128]{1,0:T(8,128)(2,1)} copy-done((bf16[2048,128]{1,0:T(8,128)(2,1)}, bf16[2048,128]{1,0:T(8,128)(2,1)S(1)}, u32[]{:S(2)}) %copy-start.2) | copy-done | bytes 524312
  70.5 0.0 copy-start.3
  70.5 0.6 copy-done.3
  71.0 5.7 %write.1 = (bf16[1536,2048]{1,0:T(8,128)(2,1)}, f32[2,768]{1,0:T(2,128)}, bf16[2048,128]{1,0:T(8,128)(2,1)}) custom-call(bf16[4,1536,512]{2,1,0:T(8,128)(2,1)} %copy-done, f32[2,768]{1,0:T(2,128)} %copy-done.3, bf16[2048,128]{1,0:T(8,128)(2,1)} %copy-done.2), custom_call_target="tpu_custom_call" | custom-call | tf_op jit(solution)/shard_map/write/pallas_call | solution.py:259
Async XLA Ops:
  0.6 1.9 %copy-start.1 = (f32[2,768,512]{2,1,0:T(8,128)S(1)}, f32[2,768,512]{2,1,0:T(8,128)}, u32[]{:S(2)}) copy-start(f32[2,768,512]{2,1,0:T(8,128)} %param.3) | copy-start | bytes 9437188
  2.5 0.7 copy-start.4
  3.2 0.7 copy-start.5
  67.0 2.7 %copy-start = (bf16[4,1536,512]{2,1,0:T(8,128)(2,1)}, bf16[4,1536,512]{2,1,0:T(8,128)(2,1)S(1)}, u32[]{:S(2)}) copy-start(bf16[4,1536,512]{2,1,0:T(8,128)(2,1)S(1)} %get-tuple-element.9.gathered) | copy-start | bytes 18874372
  69.6 0.8 %copy-start.2 = (bf16[2048,128]{1,0:T(8,128)(2,1)}, bf16[2048,128]{1,0:T(8,128)(2,1)S(1)}, u32[]{:S(2)}) copy-start(bf16[2048,128]{1,0:T(8,128)(2,1)S(1)} %get-tuple-element.11.router) | copy-start | bytes 1572868
  70.5 0.6 copy-start.3

commit v2 on v1

--- a/solution.py
+++ b/solution.py
@@ -254,7 +254,7 @@
             dma((HALF,)), dma((HALF,)), dma((HALF,)), dma((HALF,)),
             dma((3,)), dma((3,)), dma(()), dma(()), dma((3,)), dma((3,)), dma((4,)), dma((4,)), dma((3,)), dma((3,)),
         ],
-        compiler_params=pltpu.CompilerParams(collective_id=0, has_side_effects=True, vmem_limit_bytes=32 << 20),
+        compiler_params=pltpu.CompilerParams(collective_id=0, has_side_effects=True, vmem_limit_bytes=52 << 20),
     )(master_down.reshape(1536, 512), router_weight.T, router_gain.reshape(1, 512))
     down, scale, router = pl.pallas_call(
         write_kernel,
@@ -267,6 +267,7 @@
         in_specs=[vmem] * 3,
         out_specs=[hbm] * 3,
         scratch_shapes=[dma((6,))],
+        compiler_params=pltpu.CompilerParams(vmem_limit_bytes=1 << 20),
     )(gathered, scale, router)
     return down.reshape(2, 768, 2048), scale, router
 

time: 77 us -> 66.6 us (0.86)
  local copies, waits for them, and re-layouts: 7.3 us -> 0 us
  Pallas kernels: 68.8 us -> 65.9 us
    unnamed x12 -> x0, local copies, waits for them, and re-layouts: 7.3 us -> none
    pallas_call x1, Pallas kernels: 5.75 us -> 2.88 us  [body(): pl.pallas_call(write_kernel, name='write', out_shape=(jax.ShapeDtypeStruc...]
where the time goes in v2:
time: 66.6 us; the launch traced here: 66.5 us
  Pallas kernels  65.9 us (99%)
    pallas_call x1, Pallas kernels, body(): pl.pallas_call(gather_kernel, name='gather', out_shape=(pltpu.VMEM((4, 15...  63 us
    pallas_call x1, Pallas kernels, body(): pl.pallas_call(write_kernel, name='write', out_shape=(jax.ShapeDtypeStruc...  2.88 us

profile of v2, /device:TPU:2, one launch (start us, length us, event | category | flops | bytes accessed | tf_op | source)
XLA Modules:
  0.0 66.5 jit_solution(7771366471240074028)
XLA Ops:
  0.6 63.0 %gather.1 = (bf16[4,1536,512]{2,1,0:T(8,128)(2,1)S(1)}, f32[2,768]{1,0:T(2,128)S(1)}, bf16[2048,128]{1,0:T(8,128)(2,1)S(1)}) custom-call(f32[1536,512]{1,0:T(8,128)} %bitcast.4, f32[2,512]{1,0:T(2,128)} %bitcast.5, f32[1,512]{1,0:T(1,128)} %bitcast.6), custom_call_target="tpu_custom_call" | custom-call | tf_op jit(solution)/shard_map/gather/pallas_call | solution.py:235
  63.7 2.9 %write.1 = (bf16[1536,2048]{1,0:T(8,128)(2,1)}, f32[2,768]{1,0:T(2,128)}, bf16[2048,128]{1,0:T(8,128)(2,1)}) custom-call(bf16[4,1536,512]{2,1,0:T(8,128)(2,1)S(1)} %get-tuple-element.9.gathered, f32[2,768]{1,0:T(2,128)S(1)} %get-tuple-element.10.scale, bf16[2048,128]{1,0:T(8,128)(2,1)S(1)} %get-tuple-element.11.router), custom_call_target="tpu_custom_call" | custom-call | tf_op jit(solution)/shard_map/write/pallas_call | solution.py:259

commit v3 on v2

--- a/solution.py
+++ b/solution.py
@@ -43,6 +43,7 @@
     rows, sums, wide, weight, gains, pieces, tall,
     load_sem, small_sem, sum_send, sum_recv, up_send, up_recv, down_send, down_recv,
     fwd_up_send, fwd_up_recv, fwd_down_send, fwd_down_recv,
+    y_ready, far_ready, other_ready,
     ry_send, ry_recv, rc_send, rc_recv, rx_send, rx_recv, zu_send, zu_recv, zd_send, zd_recv,
 ):
     z, x, core, y = (lax.axis_index(a) for a in ("z", "x", "core", "shard"))
@@ -73,9 +74,26 @@
         copy.start()
 
     barrier = pltpu.get_barrier_semaphore()
-    peers = [at_y(1), at_y(2), at_y(3), at_x(1), at_x(2), at_x(3), partner, at_z(1), at_z(nz - 1)]
-    for peer in peers:
-        pl.semaphore_signal(barrier, inc=1, device_id=peer, device_id_type=MESH)
+    even = lax.rem(x + y + z + core, 2) == 0
+    odd = jnp.logical_not(even)
+    beside = [at_y(1), at_y(ny - 1)]
+    others = [at_z(1), at_z(nz - 1), at_x(1), at_x(nx - 1), partner]
+
+    def tell(semaphore, peers):
+        for peer in peers:
+            pl.semaphore_signal(semaphore, inc=1, device_id=peer, device_id_type=MESH)
+
+    @pl.when(even)
+    def _():
+        tell(barrier, others)
+        pl.semaphore_wait(barrier, len(beside))
+        tell(y_ready, beside)
+
+    @pl.when(odd)
+    def _():
+        tell(barrier, beside)
+        pl.semaphore_wait(y_ready, len(beside))
+        tell(far_ready, beside[1:])
 
     def remote(src, dst, send, recv, peer):
         copy = pltpu.make_async_remote_copy(
@@ -96,6 +114,12 @@
     def send_sums(first, count, slot):
         out = []
         for d in (1, 3, 2):
+            if d == 2 and slot == 0:
+
+                @pl.when(even)
+                def _():
+                    pl.semaphore_wait(far_ready, 1)
+
             view = sums.at[y, pl.ds(first, count)]
             out.append(remote(view, view, sum_send.at[slot, d - 1], sum_recv.at[slot, d - 1], at_y(d)))
             out[-1].start()
@@ -105,7 +129,6 @@
     for copy in small:
         copy.wait()
     pieces[y, mine] = (weight[...] * gains[...]).astype(BF16)
-    pl.semaphore_wait(barrier, len(peers))
     sum_copies = [send_sums(0, 1, 0)]
     partial_sums(1)
     partial_sums(2)
@@ -147,6 +170,16 @@
     for copy in ry:
         copy.wait_recv()
     view = pieces.at[:, mine]
+
+    @pl.when(even)
+    def _():
+        pl.semaphore_wait(other_ready, len(others))
+
+    @pl.when(odd)
+    def _():
+        pl.semaphore_wait(barrier, len(others))
+        tell(other_ready, others)
+
     rc = remote(view, view, rc_send, rc_recv, partner)
     rc.start()
     scales = [wide[p] for p in range(len(PARTS))]
@@ -156,11 +189,15 @@
         scale_out[block // 6 : block // 6 + 1, (block % 6) * 128 : (block % 6 + 1) * 128] = line
     rc.wait_recv()
     view = pieces.at[:, pl.ds(z * 8 + x * 2, 2)]
-    rx = [remote(view, view, rx_send.at[d - 1], rx_recv.at[d - 1], at_x(d)) for d in (1, 2, 3)]
+    rx = [remote(view, view, rx_send.at[k], rx_recv.at[k], at_x((1, nx - 1)[k])) for k in range(2)]
     for copy in rx:
         copy.start()
-    for copy in rx:
-        copy.wait_recv()
+    rx[0].wait_recv()
+    view = pieces.at[:, pl.ds(z * 8 + lax.rem(x + nx - 1, nx) * 2, 2)]
+    rx.append(remote(view, view, rx_send.at[2], rx_recv.at[2], at_x(1)))
+    rx[2].start()
+    rx[1].wait_recv()
+    rx[2].wait_recv()
     zu, zd = [], []
     for k in range(4):
         if k:
@@ -217,10 +254,14 @@
 
 def write_kernel(gathered, scale, router, down_out, scale_out, router_out, sems):
     copies = [
-        pltpu.make_async_copy(gathered.at[s], down_out.at[:, pl.ds(s * 512, 512)], sems.at[s]) for s in range(4)
+        pltpu.make_async_copy(
+            gathered.at[s, pl.ds(r * 384, 384)], down_out.at[pl.ds(r * 384, 384), pl.ds(s * 512, 512)], sems.at[s, r]
+        )
+        for r in range(4)
+        for s in range(4)
     ]
-    copies.append(pltpu.make_async_copy(scale, scale_out, sems.at[4]))
-    copies.append(pltpu.make_async_copy(router, router_out, sems.at[5]))
+    copies.append(pltpu.make_async_copy(scale, scale_out, sems.at[4, 0]))
+    copies.append(pltpu.make_async_copy(router, router_out, sems.at[4, 1]))
     for copy in copies:
         copy.start()
     for copy in copies:
@@ -228,7 +269,7 @@
 
 
 def body(master_down, router_weight, router_gain):
-    dma = pltpu.SemaphoreType.DMA
+    dma, regular = pltpu.SemaphoreType.DMA, pltpu.SemaphoreType.REGULAR
     n = len(CHUNKS)
     hbm = pl.BlockSpec(memory_space=pltpu.HBM)
     vmem = pl.BlockSpec(memory_space=pltpu.VMEM)
@@ -252,6 +293,7 @@
             pltpu.VMEM((128, 2048), F32),
             dma((3,)), dma((2,)), dma((2, 3)), dma((2, 3)), dma((n,)), dma((n,)), dma((n,)), dma((n,)),
             dma((HALF,)), dma((HALF,)), dma((HALF,)), dma((HALF,)),
+            regular, regular, regular,
             dma((3,)), dma((3,)), dma(()), dma(()), dma((3,)), dma((3,)), dma((4,)), dma((4,)), dma((3,)), dma((3,)),
         ],
         compiler_params=pltpu.CompilerParams(collective_id=0, has_side_effects=True, vmem_limit_bytes=52 << 20),
@@ -266,7 +308,7 @@
         ),
         in_specs=[vmem] * 3,
         out_specs=[hbm] * 3,
-        scratch_shapes=[dma((6,))],
+        scratch_shapes=[dma((5, 4))],
         compiler_params=pltpu.CompilerParams(vmem_limit_bytes=1 << 20),
     )(gathered, scale, router)
     return down.reshape(2, 768, 2048), scale, router

time: 66.6 us -> 64.5 us (0.968)
  Pallas kernels: 65.9 us -> 63.6 us
    pallas_call x1, Pallas kernels: 63 us -> 60.6 us  [body(): pl.pallas_call(gather_kernel, name='gather', out_shape=(pltpu.VMEM((4, 15...]
where the time goes in v3:
time: 64.5 us; the launch traced here: 64.2 us
  Pallas kernels  63.6 us (99%)
    pallas_call x1, Pallas kernels, body(): pl.pallas_call(gather_kernel, name='gather', out_shape=(pltpu.VMEM((4, 15...  60.6 us
    pallas_call x1, Pallas kernels, body(): pl.pallas_call(write_kernel, name='write', out_shape=(jax.ShapeDtypeStruc...  2.99 us

profile of v3, /device:TPU:2, one launch (start us, length us, event | category | flops | bytes accessed | tf_op | source)
XLA Modules:
  0.0 64.2 jit_solution(7201148914370044075)
XLA Ops:
  0.6 60.6 %gather.1 = (bf16[4,1536,512]{2,1,0:T(8,128)(2,1)S(1)}, f32[2,768]{1,0:T(2,128)S(1)}, bf16[2048,128]{1,0:T(8,128)(2,1)S(1)}) custom-call(f32[1536,512]{1,0:T(8,128)} %bitcast.4, f32[2,512]{1,0:T(2,128)} %bitcast.5, f32[1,512]{1,0:T(1,128)} %bitcast.6), custom_call_target="tpu_custom_call" | custom-call | tf_op jit(solution)/shard_map/gather/pallas_call | solution.py:276
  61.2 3.0 %write.1 = (bf16[1536,2048]{1,0:T(8,128)(2,1)}, f32[2,768]{1,0:T(2,128)}, bf16[2048,128]{1,0:T(8,128)(2,1)}) custom-call(bf16[4,1536,512]{2,1,0:T(8,128)(2,1)S(1)} %get-tuple-element.9.gathered, f32[2,768]{1,0:T(2,128)S(1)} %get-tuple-element.10.scale, bf16[2048,128]{1,0:T(8,128)(2,1)S(1)} %get-tuple-element.11.router), custom_call_target="tpu_custom_call" | custom-call | tf_op jit(solution)/shard_map/write/pallas_call | solution.py:301

commit v4 on v3

--- a/solution.py
+++ b/solution.py
@@ -43,7 +43,7 @@
     rows, sums, wide, weight, gains, pieces, tall,
     load_sem, small_sem, sum_send, sum_recv, up_send, up_recv, down_send, down_recv,
     fwd_up_send, fwd_up_recv, fwd_down_send, fwd_down_recv,
-    y_ready, far_ready, other_ready,
+    group_ready, other_ready,
     ry_send, ry_recv, rc_send, rc_recv, rx_send, rx_recv, zu_send, zu_recv, zd_send, zd_recv,
 ):
     z, x, core, y = (lax.axis_index(a) for a in ("z", "x", "core", "shard"))
@@ -74,26 +74,19 @@
         copy.start()
 
     barrier = pltpu.get_barrier_semaphore()
-    even = lax.rem(x + y + z + core, 2) == 0
-    odd = jnp.logical_not(even)
-    beside = [at_y(1), at_y(ny - 1)]
+    gateway = y == ny - 1
+    ordinary = y < ny - 1
     others = [at_z(1), at_z(nz - 1), at_x(1), at_x(nx - 1), partner]
 
     def tell(semaphore, peers):
         for peer in peers:
             pl.semaphore_signal(semaphore, inc=1, device_id=peer, device_id_type=MESH)
 
-    @pl.when(even)
-    def _():
-        tell(barrier, others)
-        pl.semaphore_wait(barrier, len(beside))
-        tell(y_ready, beside)
-
-    @pl.when(odd)
-    def _():
-        tell(barrier, beside)
-        pl.semaphore_wait(y_ready, len(beside))
-        tell(far_ready, beside[1:])
+    for d in (1, 2, 3):
+
+        @pl.when(y + d != ny - 1)
+        def _(d=d):
+            tell(barrier, [at_y(d)])
 
     def remote(src, dst, send, recv, peer):
         copy = pltpu.make_async_remote_copy(
@@ -114,12 +107,6 @@
     def send_sums(first, count, slot):
         out = []
         for d in (1, 3, 2):
-            if d == 2 and slot == 0:
-
-                @pl.when(even)
-                def _():
-                    pl.semaphore_wait(far_ready, 1)
-
             view = sums.at[y, pl.ds(first, count)]
             out.append(remote(view, view, sum_send.at[slot, d - 1], sum_recv.at[slot, d - 1], at_y(d)))
             out[-1].start()
@@ -129,6 +116,20 @@
     for copy in small:
         copy.wait()
     pieces[y, mine] = (weight[...] * gains[...]).astype(BF16)
+
+    @pl.when(ordinary)
+    def _():
+        pl.semaphore_wait(barrier, ny - 1)
+
+    @pl.when(y == 0)
+    def _():
+        tell(group_ready, [at_y(ny - 1)])
+
+    @pl.when(gateway)
+    def _():
+        pl.semaphore_wait(group_ready, 1)
+        tell(barrier, others)
+
     sum_copies = [send_sums(0, 1, 0)]
     partial_sums(1)
     partial_sums(2)
@@ -171,14 +172,14 @@
         copy.wait_recv()
     view = pieces.at[:, mine]
 
-    @pl.when(even)
-    def _():
-        pl.semaphore_wait(other_ready, len(others))
-
-    @pl.when(odd)
+    @pl.when(gateway)
     def _():
         pl.semaphore_wait(barrier, len(others))
-        tell(other_ready, others)
+        tell(other_ready, [at_y(d) for d in (1, 2, 3)])
+
+    @pl.when(ordinary)
+    def _():
+        pl.semaphore_wait(other_ready, 1)
 
     rc = remote(view, view, rc_send, rc_recv, partner)
     rc.start()
@@ -255,9 +256,9 @@
 def write_kernel(gathered, scale, router, down_out, scale_out, router_out, sems):
     copies = [
         pltpu.make_async_copy(
-            gathered.at[s, pl.ds(r * 384, 384)], down_out.at[pl.ds(r * 384, 384), pl.ds(s * 512, 512)], sems.at[s, r]
+            gathered.at[s, pl.ds(r * 768, 768)], down_out.at[pl.ds(r * 768, 768), pl.ds(s * 512, 512)], sems.at[s, r]
         )
-        for r in range(4)
+        for r in range(2)
         for s in range(4)
     ]
     copies.append(pltpu.make_async_copy(scale, scale_out, sems.at[4, 0]))
@@ -293,7 +294,7 @@
             pltpu.VMEM((128, 2048), F32),
             dma((3,)), dma((2,)), dma((2, 3)), dma((2, 3)), dma((n,)), dma((n,)), dma((n,)), dma((n,)),
             dma((HALF,)), dma((HALF,)), dma((HALF,)), dma((HALF,)),
-            regular, regular, regular,
+            regular, regular,
             dma((3,)), dma((3,)), dma(()), dma(()), dma((3,)), dma((3,)), dma((4,)), dma((4,)), dma((3,)), dma((3,)),
         ],
         compiler_params=pltpu.CompilerParams(collective_id=0, has_side_effects=True, vmem_limit_bytes=52 << 20),

time: 64.5 us -> 63.6 us (0.986)
  Pallas kernels: 63.6 us -> 62.9 us
    pallas_call x1, Pallas kernels: 60.6 us -> 59.9 us  [body(): pl.pallas_call(gather_kernel, name='gather', out_shape=(pltpu.VMEM((4, 15...]
where the time goes in v4:
time: 63.6 us; the launch traced here: 63.5 us
  Pallas kernels  62.9 us (99%)
  between operations  0.64 us (1%)
    pallas_call x1, Pallas kernels, body(): pl.pallas_call(gather_kernel, name='gather', out_shape=(pltpu.VMEM((4, 15...  59.9 us
    pallas_call x1, Pallas kernels, body(): pl.pallas_call(write_kernel, name='write', out_shape=(jax.ShapeDtypeStruc...  3 us

profile of v4, /device:TPU:2, one launch (start us, length us, event | category | flops | bytes accessed | tf_op | source)
XLA Modules:
  0.0 63.5 jit_solution(14566086468091700625)
XLA Ops:
  0.6 59.9 %gather.1 = (bf16[4,1536,512]{2,1,0:T(8,128)(2,1)S(1)}, f32[2,768]{1,0:T(2,128)S(1)}, bf16[2048,128]{1,0:T(8,128)(2,1)S(1)}) custom-call(f32[1536,512]{1,0:T(8,128)} %bitcast.4, f32[2,512]{1,0:T(2,128)} %bitcast.5, f32[1,512]{1,0:T(1,128)} %bitcast.6), custom_call_target="tpu_custom_call" | custom-call | tf_op jit(solution)/shard_map/gather/pallas_call | solution.py:277
  60.5 3.0 %write.1 = (bf16[1536,2048]{1,0:T(8,128)(2,1)}, f32[2,768]{1,0:T(2,128)}, bf16[2048,128]{1,0:T(8,128)(2,1)}) custom-call(bf16[4,1536,512]{2,1,0:T(8,128)(2,1)S(1)} %get-tuple-element.9.gathered, f32[2,768]{1,0:T(2,128)S(1)} %get-tuple-element.10.scale, bf16[2048,128]{1,0:T(8,128)(2,1)S(1)} %get-tuple-element.11.router), custom_call_target="tpu_custom_call" | custom-call | tf_op jit(solution)/shard_map/write/pallas_call | solution.py:302

commit v5 on v2

v5 whole, which is shorter than its diff:
```python
import jax
import jax.numpy as jnp
from jax import lax
from jax.experimental import pallas as pl
from jax.experimental.pallas import tpu as pltpu
from jax.sharding import Mesh
from jax.sharding import PartitionSpec as P

MESH = pl.DeviceIdType.MESH
EXPERT = ("z", "x", "core")
BF16, F32 = jnp.bfloat16, jnp.float32

BLOCK = 128
GROUPS = BLOCK // 8
PARTS = ((0, 2), (2, 7), (7, 12))
CHUNKS = ((0, 1), (1, 2), (2, 6), (6, 12))
UP_ORDER, DOWN_ORDER = (0, 1, 2, 3), (0, 1, 3, 2)
HALF = 768
RAW = 48


def part_of(block):
    for p, (lo, hi) in enumerate(PARTS):
        if lo <= block < hi:
            return p, (block - lo) * GROUPS


def pick(first):
    lane = lax.broadcasted_iota(jnp.int32, (GROUPS, 8, 128), 2)
    group = lax.broadcasted_iota(jnp.int32, (GROUPS, 8, 128), 0)
    return lane == group + first


def column(packed, block):
    p, first = part_of(block)
    spread = jnp.where(pick(first), packed[p][None], 0.0)
    return jnp.sum(spread, axis=2, keepdims=True).reshape(BLOCK, 1)


def done(view, semaphore):
    pltpu.make_async_copy(view, view, semaphore).wait()


def gather_kernel(
    master, router, gain,
    gathered, scale_out, router_out,
    rows, raw, sums, wide, weight, gains, pieces, tall,
    load_sem, small_sem, sum_send, sum_recv, raw_send, raw_recv,
    up_send, down_send, up_recv, down_recv, group_ready, other_ready,
    row_send, row_recv, col_send, rc_recv, rx_recv, zu_recv, zd_recv,
):
    z, x, core, y = (lax.axis_index(a) for a in ("z", "x", "core", "shard"))
    nz, nx, ny = 8, 4, 4
    mine = z * (nx * 2) + x * 2 + core
    below, above = lax.rem(y + ny - 1, ny), lax.rem(y + 1, ny)
    first_raw = 12 * BLOCK - RAW

    def at_y(step):
        return (z, x, core, lax.rem(y + step, ny))

    def at_x(step):
        return (z, lax.rem(x + step, nx), core, y)

    def at_z(step):
        return (lax.rem(z + step, nz), x, core, y)

    partner = (z, x, 1 - core, y)

    def tell(semaphore, peers):
        for peer in peers:
            pl.semaphore_signal(semaphore, inc=1, device_id=peer, device_id_type=MESH)

    def send(src, dst, send_sem, recv_sem, peer):
        pltpu.make_async_remote_copy(
            src_ref=src, dst_ref=dst, send_sem=send_sem, recv_sem=recv_sem, device_id=peer, device_id_type=MESH
        ).start()

    barrier = pltpu.get_barrier_semaphore()
    gateway = y == ny - 1
    ordinary = y < ny - 1
    others = [at_z(1), at_z(nz - 1), at_x(1), at_x(nx - 1), partner]
    for d in (1, 3, 2):

        @pl.when(y + d != ny - 1)
        def _(d=d):
            tell(barrier, [at_y(d)])

    def load(at, count, k):
        view = pl.ds(at, count)
        return pltpu.make_async_copy(master.at[view], rows.at[view], load_sem.at[k])

    small = [
        pltpu.make_async_copy(router, weight, small_sem.at[0]),
        pltpu.make_async_copy(gain, gains, small_sem.at[1]),
    ]
    loads = [load(0, 256, 0), load(first_raw, RAW, 1), load(256, first_raw - 256, 2)]
    loads[0].start()
    loads[1].start()
    for copy in small:
        copy.start()
    loads[2].start()

    @pl.when(ordinary)
    def _():
        pl.semaphore_wait(barrier, ny - 1)

    @pl.when(y == ny - 2)
    def _():
        tell(group_ready, [at_y(1)])

    def partial_sums(p):
        lo, hi = PARTS[p]
        packed = jnp.zeros((8, 128), F32)
        for block in range(lo, hi):
            values = rows[pl.ds(block * BLOCK, BLOCK), :]
            total = jnp.sum(values * values, axis=1, keepdims=True).reshape(GROUPS, 8, 1)
            packed = packed + jnp.sum(jnp.where(pick((block - lo) * GROUPS), total, 0.0), axis=0)
        sums[y, p] = packed

    def send_sums(first, count, slot):
        view = sums.at[y, pl.ds(first, count)]
        for d in (2, 1, 3):
            send(view, view, sum_send, sum_recv.at[slot], at_y(d))

    loads[0].wait()
    partial_sums(0)

    @pl.when(gateway)
    def _():
        pl.semaphore_wait(group_ready, 1)

    send_sums(0, 1, 0)
    loads[1].wait()
    view = rows.at[pl.ds(first_raw, RAW)]
    send(view, raw.at[0], raw_send, raw_recv, at_y(1))
    send(view, raw.at[1], raw_send, raw_recv, at_y(ny - 1))

    @pl.when(gateway)
    def _():
        tell(barrier, others)

    loads[2].wait()
    partial_sums(1)
    partial_sums(2)
    send_sums(1, 2, 1)

    for copy in small:
        copy.wait()
    pieces[y, mine] = (weight[...] * gains[...]).astype(BF16)
    view = pieces.at[y, mine]
    for d in (1, 2, 3):
        send(view, view, row_send, row_recv, at_y(d))

    inverse = {}

    def finish_sums(slot, parts):
        done(sums.at[pl.ds(0, ny - 1), pl.ds(parts[0], len(parts))], sum_recv.at[slot])
        for p in parts:
            scale = jnp.sqrt((sums[0, p] + sums[1, p]) + (sums[2, p] + sums[3, p]))
            wide[p] = scale
            inverse[p] = 1.0 / scale

    def rescale(c):
        for block in range(*CHUNKS[c]):
            view = pl.ds(block * BLOCK, BLOCK)
            gathered[y, view, :] = (rows[view, :] * column(inverse, block)).astype(BF16)

    def send_chunk(c, upwards):
        lo, hi = CHUNKS[c][0] * BLOCK, min(CHUNKS[c][1] * BLOCK, first_raw)
        view = gathered.at[y, pl.ds(lo, hi - lo)]
        onwards = (hi <= HALF) == upwards
        k = 0 if onwards else 1
        if upwards:
            send(view, view, up_send, up_recv.at[k], at_y(1))
        else:
            send(view, view, down_send, down_recv.at[k], at_y(ny - 1))

    finish_sums(0, (0,))
    for c in (0, 1):
        rescale(c)
        send_chunk(c, True)
        send_chunk(c, False)
    finish_sums(1, (1, 2))
    rescale(2)
    send_chunk(2, True)
    rescale(3)
    send_chunk(3, False)
    send_chunk(3, True)
    send_chunk(2, False)

    done(raw, raw_recv)
    last = column(inverse, 11)[BLOCK - RAW :]
    for k, owner in enumerate((below, above)):
        gathered[owner, pl.ds(first_raw, RAW), :] = (raw[k] * last).astype(BF16)

    done(pieces.at[pl.ds(0, ny - 1), 0], row_recv)
    scales = [wide[p] for p in range(len(PARTS))]
    for block in range(12):
        same = lax.broadcasted_iota(jnp.int32, (BLOCK, 128), 0) == lax.broadcasted_iota(jnp.int32, (BLOCK, 128), 1)
        line = jnp.sum(jnp.where(same, column(scales, block), 0.0), axis=0, keepdims=True)
        scale_out[block // 6 : block // 6 + 1, (block % 6) * 128 : (block % 6 + 1) * 128] = line

    @pl.when(gateway)
    def _():
        pl.semaphore_wait(barrier, len(others))
        tell(other_ready, [at_y(d) for d in (1, 2, 3)])

    @pl.when(ordinary)
    def _():
        pl.semaphore_wait(other_ready, 1)

    view = pieces.at[:, mine]
    send(view, view, col_send, rc_recv, partner)
    done(view, rc_recv)
    view = pieces.at[:, pl.ds(z * 8 + x * 2, 2)]
    send(view, view, col_send, rx_recv.at[0], at_x(1))
    send(view, view, col_send, rx_recv.at[1], at_x(nx - 1))
    done(view, rx_recv.at[0])
    view = pieces.at[:, pl.ds(z * 8 + lax.rem(x + nx - 1, nx) * 2, 2)]
    send(view, view, col_send, rx_recv.at[1], at_x(1))
    done(pieces.at[:, pl.ds(0, 4)], rx_recv.at[1])

    def plane(step):
        return pieces.at[:, pl.ds(lax.rem(z + step, nz) * 8, 8)]

    for k in range(4):
        if k:
            done(plane(0), zu_recv.at[k - 1])
        send(plane(nz - k), plane(nz - k), col_send, zu_recv.at[k], at_z(1))
        if k < 3:
            if k:
                done(plane(0), zd_recv.at[k - 1])
            send(plane(k), plane(k), col_send, zd_recv.at[k], at_z(nz - 1))

    view = gathered.at[below, pl.ds(0, HALF)]
    done(view, up_recv.at[0])
    send(view, view, up_send, up_recv.at[2], at_y(1))
    view = gathered.at[above, pl.ds(HALF, 12 * BLOCK - HALF)]
    done(gathered.at[0, pl.ds(0, first_raw - HALF)], down_recv.at[0])
    send(view, view, down_send, down_recv.at[2], at_y(ny - 1))

    done(plane(0), zu_recv.at[3])
    done(plane(0), zd_recv.at[2])

    def lay(step, _):
        for s in range(ny):
            four = [pieces[s, step * 4 + i].astype(F32) for i in range(4)]
            tall[pl.ds(pl.multiple_of(step * 8, 8), 8), s * 512 : (s + 1) * 512] = jnp.concatenate(four, axis=0)
        return 0

    lax.fori_loop(0, 16, lay, 0)
    for i in range(16):
        router_out[i * 128 : (i + 1) * 128, :] = tall[:, i * 128 : (i + 1) * 128].T.astype(BF16)

    done(sums.at[pl.ds(0, ny - 1)], sum_send)
    done(raw, raw_send)
    done(pieces.at[pl.ds(0, ny - 1), 0], row_send)
    done(pieces.at[:, pl.ds(0, 63)], col_send)
    done(gathered.at[0, pl.ds(0, first_raw - HALF)], up_recv.at[1])
    done(gathered.at[0, pl.ds(0, HALF)], down_recv.at[1])
    sent = gathered.at[pl.ds(0, 2), pl.ds(0, (first_raw + HALF) // 2)]
    done(sent, up_send)
    done(sent, down_send)
    done(gathered.at[0, pl.ds(0, HALF)], up_recv.at[2])
    done(gathered.at[0, pl.ds(0, 12 * BLOCK - HALF)], down_recv.at[2])


def write_kernel(gathered, scale, router, down_out, scale_out, router_out, sems):
    copies = [
        pltpu.make_async_copy(gathered.at[s], down_out.at[:, pl.ds(s * 512, 512)], sems.at[0]) for s in range(4)
    ]
    copies.append(pltpu.make_async_copy(scale, scale_out, sems.at[1]))
    copies.append(pltpu.make_async_copy(router, router_out, sems.at[2]))
    for copy in copies:
        copy.start()
    done(down_out, sems.at[0])
    copies[4].wait()
    copies[5].wait()


def body(master_down, router_weight, router_gain):
    dma, regular = pltpu.SemaphoreType.DMA, pltpu.SemaphoreType.REGULAR
    hbm = pl.BlockSpec(memory_space=pltpu.HBM)
    vmem = pl.BlockSpec(memory_space=pltpu.VMEM)
    gathered, scale, router = pl.pallas_call(
        gather_kernel,
        name="gather",
        out_shape=(
            pltpu.VMEM((4, 1536, 512), BF16),
            pltpu.VMEM((2, 768), F32),
            pltpu.VMEM((2048, 128), BF16),
        ),
        in_specs=[hbm] * 3,
        out_specs=[vmem] * 3,
        scratch_shapes=[
            pltpu.VMEM((1536, 512), F32),
            pltpu.VMEM((2, RAW, 512), F32),
            pltpu.VMEM((4, 3, 8, 128), F32),
            pltpu.VMEM((3, 8, 128), F32),
            pltpu.VMEM((2, 512), F32),
            pltpu.VMEM((1, 512), F32),
            pltpu.VMEM((4, 64, 2, 512), BF16),
            pltpu.VMEM((128, 2048), F32),
            dma((3,)), dma((2,)), dma(()), dma((2,)), dma(()), dma(()),
            dma(()), dma(()), dma((3,)), dma((3,)), regular, regular,
            dma(()), dma(()), dma(()), dma(()), dma((2,)), dma((4,)), dma((3,)),
        ],
        compiler_params=pltpu.CompilerParams(collective_id=0, has_side_effects=True, vmem_limit_bytes=52 << 20),
    )(master_down.reshape(1536, 512), router_weight.T, router_gain.reshape(1, 512))
    down, scale, router = pl.pallas_call(
        write_kernel,
        name="write",
        out_shape=(
            jax.ShapeDtypeStruct((1536, 2048), BF16),
            jax.ShapeDtypeStruct((2, 768), F32),
            jax.ShapeDtypeStruct((2048, 128), BF16),
        ),
        in_specs=[vmem] * 3,
        out_specs=[hbm] * 3,
        scratch_shapes=[dma((3,))],
        compiler_params=pltpu.CompilerParams(vmem_limit_bytes=1 << 20),
    )(gathered, scale, router)
    return down.reshape(2, 768, 2048), scale, router


def solution(mesh):
    finer = Mesh(mesh.devices.reshape(8, 4, 2, mesh.shape["shard"]), (*EXPERT, "shard"))
    in_specs = (P(EXPERT, None, "shard"), P("shard", EXPERT), P("shard"))
    out_specs = (P(EXPERT, None, None), P(EXPERT, None), P())
    return jax.shard_map(body, mesh=finer, in_specs=in_specs, out_specs=out_specs, check_vma=False)
```

time: 66.6 us -> 62 us (0.931)
  Pallas kernels: 65.9 us -> 60.8 us
    pallas_call x1, Pallas kernels: 63 us -> 58 us  [body(): pl.pallas_call(gather_kernel, name='gather', out_shape=(pltpu.VMEM((4, 15...]
where the time goes in v5:
time: 62 us; the launch traced here: 61.5 us
  Pallas kernels  60.8 us (98%)
  between operations  0.64 us (1%)
    pallas_call x1, Pallas kernels, body(): pl.pallas_call(gather_kernel, name='gather', out_shape=(pltpu.VMEM((4, 15...  58 us
    pallas_call x1, Pallas kernels, body(): pl.pallas_call(write_kernel, name='write', out_shape=(jax.ShapeDtypeStruc...  2.85 us

profile of v5, /device:TPU:2, one launch (start us, length us, event | category | flops | bytes accessed | tf_op | source)
XLA Modules:
  0.0 61.5 jit_solution(6956523099708140248)
XLA Ops:
  0.6 58.0 %gather.1 = (bf16[4,1536,512]{2,1,0:T(8,128)(2,1)S(1)}, f32[2,768]{1,0:T(2,128)S(1)}, bf16[2048,128]{1,0:T(8,128)(2,1)S(1)}) custom-call(f32[1536,512]{1,0:T(8,128)} %bitcast.4, f32[2,512]{1,0:T(2,128)} %bitcast.5, f32[1,512]{1,0:T(1,128)} %bitcast.6), custom_call_target="tpu_custom_call" | custom-call | tf_op jit(solution)/shard_map/gather/pallas_call | solution.py:285
  58.6 2.9 %write.1 = (bf16[1536,2048]{1,0:T(8,128)(2,1)}, f32[2,768]{1,0:T(2,128)}, bf16[2048,128]{1,0:T(8,128)(2,1)}) custom-call(bf16[4,1536,512]{2,1,0:T(8,128)(2,1)S(1)} %get-tuple-element.9.gathered, f32[2,768]{1,0:T(2,128)S(1)} %get-tuple-element.10.scale, bf16[2048,128]{1,0:T(8,128)(2,1)S(1)} %get-tuple-element.11.router), custom_call_target="tpu_custom_call" | custom-call | tf_op jit(solution)/shard_map/write/pallas_call | solution.py:310

commit v6 on v5

--- a/solution.py
+++ b/solution.py
@@ -16,7 +16,8 @@
 CHUNKS = ((0, 1), (1, 2), (2, 6), (6, 12))
 UP_ORDER, DOWN_ORDER = (0, 1, 2, 3), (0, 1, 3, 2)
 HALF = 768
-RAW = 48
+SHIFT = 32
+RAW = 32
 
 
 def part_of(block):
@@ -232,9 +233,15 @@
                 done(plane(0), zd_recv.at[k - 1])
             send(plane(k), plane(k), col_send, zd_recv.at[k], at_z(nz - 1))
 
-    view = gathered.at[below, pl.ds(0, HALF)]
-    done(view, up_recv.at[0])
+    done(gathered.at[0, pl.ds(0, HALF)], up_recv.at[0])
+    view = gathered.at[below, pl.ds(0, HALF - SHIFT)]
     send(view, view, up_send, up_recv.at[2], at_y(1))
+
+    @pl.when(y < ny - 1)
+    def _():
+        view = gathered.at[below, pl.ds(HALF - SHIFT, SHIFT)]
+        send(view, view, up_send, up_recv.at[2], at_y(1))
+
     view = gathered.at[above, pl.ds(HALF, 12 * BLOCK - HALF)]
     done(gathered.at[0, pl.ds(0, first_raw - HALF)], down_recv.at[0])
     send(view, view, down_send, down_recv.at[2], at_y(ny - 1))
@@ -258,11 +265,45 @@
     done(pieces.at[:, pl.ds(0, 63)], col_send)
     done(gathered.at[0, pl.ds(0, first_raw - HALF)], up_recv.at[1])
     done(gathered.at[0, pl.ds(0, HALF)], down_recv.at[1])
-    sent = gathered.at[pl.ds(0, 2), pl.ds(0, (first_raw + HALF) // 2)]
-    done(sent, up_send)
-    done(sent, down_send)
-    done(gathered.at[0, pl.ds(0, HALF)], up_recv.at[2])
-    done(gathered.at[0, pl.ds(0, 12 * BLOCK - HALF)], down_recv.at[2])
+
+    @pl.when(y == 1)
+    def _():
+        view = gathered.at[above, pl.ds(HALF - SHIFT, SHIFT)]
+        send(view, view, down_send, down_recv.at[2], at_y(ny - 1))
+
+    def both(count):
+        return gathered.at[pl.ds(0, 2), pl.ds(0, count // 2)]
+
+    plain = first_raw + HALF
+    last_ones = 12 * BLOCK - HALF
+
+    @pl.when(y == 0)
+    def _():
+        done(both(plain), up_send)
+        done(both(plain), down_send)
+        done(gathered.at[0, pl.ds(0, last_ones + SHIFT)], down_recv.at[2])
+        done(gathered.at[0, pl.ds(0, HALF - SHIFT)], up_recv.at[2])
+
+    @pl.when(y > 0)
+    def _():
+        @pl.when(y == 1)
+        def _():
+            done(both(plain + SHIFT), down_send)
+
+        @pl.when(y > 1)
+        def _():
+            done(both(plain), down_send)
+
+        @pl.when(y == ny - 1)
+        def _():
+            done(both(plain - SHIFT), up_send)
+
+        @pl.when(y < ny - 1)
+        def _():
+            done(both(plain), up_send)
+
+        done(gathered.at[0, pl.ds(0, HALF)], up_recv.at[2])
+        done(gathered.at[0, pl.ds(0, last_ones)], down_recv.at[2])
 
 
 def write_kernel(gathered, scale, router, down_out, scale_out, router_out, sems):

time: 62 us -> 61.5 us (level)
  no operation moved by 1% of the time
where the time goes in v6:
time: 61.5 us; the launch traced here: 61.4 us
  Pallas kernels  60.7 us (99%)
  between operations  0.64 us (1%)
    pallas_call x1, Pallas kernels, body(): pl.pallas_call(gather_kernel, name='gather', out_shape=(pltpu.VMEM((4, 15...  57.9 us
    pallas_call x1, Pallas kernels, body(): pl.pallas_call(write_kernel, name='write', out_shape=(jax.ShapeDtypeStruc...  2.85 us

profile of v6, /device:TPU:2, one launch (start us, length us, event | category | flops | bytes accessed | tf_op | source)
XLA Modules:
  0.0 61.4 jit_solution(17757543940771286896)
XLA Ops:
  0.6 57.9 %gather.1 = (bf16[4,1536,512]{2,1,0:T(8,128)(2,1)S(1)}, f32[2,768]{1,0:T(2,128)S(1)}, bf16[2048,128]{1,0:T(8,128)(2,1)S(1)}) custom-call(f32[1536,512]{1,0:T(8,128)} %bitcast.4, f32[2,512]{1,0:T(2,128)} %bitcast.5, f32[1,512]{1,0:T(1,128)} %bitcast.6), custom_call_target="tpu_custom_call" | custom-call | tf_op jit(solution)/shard_map/gather/pallas_call | solution.py:326
  58.5 2.9 %write.1 = (bf16[1536,2048]{1,0:T(8,128)(2,1)}, f32[2,768]{1,0:T(2,128)}, bf16[2048,128]{1,0:T(8,128)(2,1)}) custom-call(bf16[4,1536,512]{2,1,0:T(8,128)(2,1)S(1)} %get-tuple-element.9.gathered, f32[2,768]{1,0:T(2,128)S(1)} %get-tuple-element.10.scale, bf16[2048,128]{1,0:T(8,128)(2,1)S(1)} %get-tuple-element.11.router), custom_call_target="tpu_custom_call" | custom-call | tf_op jit(solution)/shard_map/write/pallas_call | solution.py:351

commit v7 on v5

--- a/solution.py
+++ b/solution.py
@@ -13,10 +13,11 @@
 BLOCK = 128
 GROUPS = BLOCK // 8
 PARTS = ((0, 2), (2, 7), (7, 12))
-CHUNKS = ((0, 1), (1, 2), (2, 6), (6, 12))
-UP_ORDER, DOWN_ORDER = (0, 1, 2, 3), (0, 1, 3, 2)
+CHUNKS = ((0, 1), (1, 2), (2, 4), (4, 12))
+LEAD = 512
 HALF = 768
-RAW = 48
+SHIFT = 32
+RAW = 32
 
 
 def part_of(block):
@@ -46,13 +47,12 @@
     gathered, scale_out, router_out,
     rows, raw, sums, wide, weight, gains, pieces, tall,
     load_sem, small_sem, sum_send, sum_recv, raw_send, raw_recv,
-    up_send, down_send, up_recv, down_recv, group_ready, other_ready,
+    lead_send, rest_send, up_recv, down_recv, group_ready, other_ready, turn,
     row_send, row_recv, col_send, rc_recv, rx_recv, zu_recv, zd_recv,
 ):
     z, x, core, y = (lax.axis_index(a) for a in ("z", "x", "core", "shard"))
     nz, nx, ny = 8, 4, 4
     mine = z * (nx * 2) + x * 2 + core
-    below, above = lax.rem(y + ny - 1, ny), lax.rem(y + 1, ny)
     first_raw = 12 * BLOCK - RAW
 
     def at_y(step):
@@ -74,6 +74,9 @@
         pltpu.make_async_remote_copy(
             src_ref=src, dst_ref=dst, send_sem=send_sem, recv_sem=recv_sem, device_id=peer, device_id_type=MESH
         ).start()
+
+    def both(count):
+        return gathered.at[pl.ds(0, 2), pl.ds(0, count)]
 
     barrier = pltpu.get_barrier_semaphore()
     gateway = y == ny - 1
@@ -163,35 +166,30 @@
     def rescale(c):
         for block in range(*CHUNKS[c]):
             view = pl.ds(block * BLOCK, BLOCK)
-            gathered[y, view, :] = (rows[view, :] * column(inverse, block)).astype(BF16)
-
-    def send_chunk(c, upwards):
+            gathered[0, view, :] = (rows[view, :] * column(inverse, block)).astype(BF16)
+
+    def send_chunk(c):
         lo, hi = CHUNKS[c][0] * BLOCK, min(CHUNKS[c][1] * BLOCK, first_raw)
-        view = gathered.at[y, pl.ds(lo, hi - lo)]
-        onwards = (hi <= HALF) == upwards
-        k = 0 if onwards else 1
-        if upwards:
-            send(view, view, up_send, up_recv.at[k], at_y(1))
-        else:
-            send(view, view, down_send, down_recv.at[k], at_y(ny - 1))
-
-    finish_sums(0, (0,))
-    for c in (0, 1):
+        here, view = gathered.at[0, pl.ds(lo, hi - lo)], pl.ds(lo, hi - lo)
+        semaphore = lead_send if hi <= LEAD else rest_send
+        send(here, gathered.at[1, view], semaphore, up_recv, at_y(1))
+        send(here, gathered.at[2, view], semaphore, down_recv, at_y(ny - 1))
+
+    for c in range(4):
+        if c == 0:
+            finish_sums(0, (0,))
+        if c == 2:
+            finish_sums(1, (1, 2))
         rescale(c)
-        send_chunk(c, True)
-        send_chunk(c, False)
-    finish_sums(1, (1, 2))
-    rescale(2)
-    send_chunk(2, True)
-    rescale(3)
-    send_chunk(3, False)
-    send_chunk(3, True)
-    send_chunk(2, False)
+
+        @pl.when(core == 1)
+        def _(c=c):
+            send_chunk(c)
 
     done(raw, raw_recv)
     last = column(inverse, 11)[BLOCK - RAW :]
-    for k, owner in enumerate((below, above)):
-        gathered[owner, pl.ds(first_raw, RAW), :] = (raw[k] * last).astype(BF16)
+    for k in range(2):
+        gathered[k + 1, pl.ds(first_raw, RAW), :] = (raw[k] * last).astype(BF16)
 
     done(pieces.at[pl.ds(0, ny - 1), 0], row_recv)
     scales = [wide[p] for p in range(len(PARTS))]
@@ -208,6 +206,17 @@
     @pl.when(ordinary)
     def _():
         pl.semaphore_wait(other_ready, 1)
+
+    @pl.when(core == 1)
+    def _():
+        done(both(LEAD), lead_send)
+        tell(turn, [partner])
+
+    @pl.when(core == 0)
+    def _():
+        pl.semaphore_wait(turn, 1)
+        for c in range(4):
+            send_chunk(c)
 
     view = pieces.at[:, mine]
     send(view, view, col_send, rc_recv, partner)
@@ -232,13 +241,6 @@
                 done(plane(0), zd_recv.at[k - 1])
             send(plane(k), plane(k), col_send, zd_recv.at[k], at_z(nz - 1))
 
-    view = gathered.at[below, pl.ds(0, HALF)]
-    done(view, up_recv.at[0])
-    send(view, view, up_send, up_recv.at[2], at_y(1))
-    view = gathered.at[above, pl.ds(HALF, 12 * BLOCK - HALF)]
-    done(gathered.at[0, pl.ds(0, first_raw - HALF)], down_recv.at[0])
-    send(view, view, down_send, down_recv.at[2], at_y(ny - 1))
-
     done(plane(0), zu_recv.at[3])
     done(plane(0), zd_recv.at[2])
 
@@ -256,26 +258,95 @@
     done(raw, raw_send)
     done(pieces.at[pl.ds(0, ny - 1), 0], row_send)
     done(pieces.at[:, pl.ds(0, 63)], col_send)
-    done(gathered.at[0, pl.ds(0, first_raw - HALF)], up_recv.at[1])
-    done(gathered.at[0, pl.ds(0, HALF)], down_recv.at[1])
-    sent = gathered.at[pl.ds(0, 2), pl.ds(0, (first_raw + HALF) // 2)]
-    done(sent, up_send)
-    done(sent, down_send)
-    done(gathered.at[0, pl.ds(0, HALF)], up_recv.at[2])
-    done(gathered.at[0, pl.ds(0, 12 * BLOCK - HALF)], down_recv.at[2])
-
-
-def write_kernel(gathered, scale, router, down_out, scale_out, router_out, sems):
-    copies = [
-        pltpu.make_async_copy(gathered.at[s], down_out.at[:, pl.ds(s * 512, 512)], sems.at[0]) for s in range(4)
-    ]
+    @pl.when(core == 0)
+    def _():
+        done(both(LEAD), lead_send)
+
+    done(both(first_raw - LEAD), rest_send)
+    done(gathered.at[0, pl.ds(0, first_raw)], up_recv)
+    done(gathered.at[0, pl.ds(0, first_raw)], down_recv)
+
+
+def write_kernel(gathered, scale, router, down_out, scale_out, router_out, same, sems):
+    y = lax.axis_index("shard")
+    copies = []
+    for k, d in enumerate((0, 3, 1)):
+        s = lax.rem(y + d, 4)
+        columns = pl.ds(pl.multiple_of(s * 512, 512), 512)
+        copies.append(pltpu.make_async_copy(gathered.at[k], down_out.at[:, columns], sems.at[0]))
     copies.append(pltpu.make_async_copy(scale, scale_out, sems.at[1]))
     copies.append(pltpu.make_async_copy(router, router_out, sems.at[2]))
     for copy in copies:
         copy.start()
-    done(down_out, sems.at[0])
+    done(down_out.at[:, pl.ds(0, 3 * 512)], sems.at[0])
+    copies[3].wait()
     copies[4].wait()
-    copies[5].wait()
+
+
+def forward_kernel(gathered, far, up_send, down_send, up_recv, down_recv):
+    z, x, core, y = (lax.axis_index(a) for a in ("z", "x", "core", "shard"))
+    ny = 4
+    up, down = (z, x, core, lax.rem(y + 1, ny)), (z, x, core, lax.rem(y + ny - 1, ny))
+    barrier = pltpu.get_barrier_semaphore()
+    for peer in (up, down):
+        pl.semaphore_signal(barrier, inc=1, device_id=peer, device_id_type=MESH)
+    pl.semaphore_wait(barrier, 2)
+
+    def send(owner, lo, hi, send_sem, recv_sem, peer):
+        pltpu.make_async_remote_copy(
+            src_ref=gathered.at[owner, pl.ds(lo, hi - lo)],
+            dst_ref=far.at[pl.ds(lo, hi - lo)],
+            send_sem=send_sem,
+            recv_sem=recv_sem,
+            device_id=peer,
+            device_id_type=MESH,
+        ).start()
+
+    end = 12 * BLOCK
+    send(1, 0, HALF - SHIFT, up_send, up_recv, up)
+    send(2, HALF, end, down_send, down_recv, down)
+
+    @pl.when(y < ny - 1)
+    def _():
+        send(1, HALF - SHIFT, HALF, up_send, up_recv, up)
+
+    @pl.when(y == 1)
+    def _():
+        send(2, HALF - SHIFT, HALF, down_send, down_recv, down)
+
+    @pl.when(y == ny - 1)
+    def _():
+        done(far.at[pl.ds(0, HALF - SHIFT)], up_send)
+
+    @pl.when(y < ny - 1)
+    def _():
+        done(far.at[pl.ds(0, HALF)], up_send)
+
+    @pl.when(y == 1)
+    def _():
+        done(far.at[pl.ds(0, end - HALF + SHIFT)], down_send)
+
+    @pl.when(y != 1)
+    def _():
+        done(far.at[pl.ds(0, end - HALF)], down_send)
+
+    @pl.when(y == 0)
+    def _():
+        done(far.at[pl.ds(0, HALF - SHIFT)], up_recv)
+        done(far.at[pl.ds(0, end - HALF + SHIFT)], down_recv)
+
+    @pl.when(y > 0)
+    def _():
+        done(far.at[pl.ds(0, HALF)], up_recv)
+        done(far.at[pl.ds(0, end - HALF)], down_recv)
+
+
+def last_kernel(down_in, far, down_out, sem):
+    s = lax.rem(lax.axis_index("shard") + 2, 4)
+    columns = pl.ds(pl.multiple_of(s * 512, 512), 512)
+    copy = pltpu.make_async_copy(far, down_out.at[:, columns], sem)
+    copy.start()
+    copy.wait()
 
 
 def body(master_down, router_weight, router_gain):
@@ -286,7 +357,7 @@
         gather_kernel,
         name="gather",
         out_shape=(
-            pltpu.VMEM((4, 1536, 512), BF16),
+            pltpu.VMEM((3, 1536, 512), BF16),
             pltpu.VMEM((2, 768), F32),
             pltpu.VMEM((2048, 128), BF16),
         ),
@@ -302,24 +373,45 @@
             pltpu.VMEM((4, 64, 2, 512), BF16),
             pltpu.VMEM((128, 2048), F32),
             dma((3,)), dma((2,)), dma(()), dma((2,)), dma(()), dma(()),
-            dma(()), dma(()), dma((3,)), dma((3,)), regular, regular,
+            dma(()), dma(()), dma(()), dma(()), regular, regular, regular,
             dma(()), dma(()), dma(()), dma(()), dma((2,)), dma((4,)), dma((3,)),
         ],
-        compiler_params=pltpu.CompilerParams(collective_id=0, has_side_effects=True, vmem_limit_bytes=52 << 20),
+        compiler_params=pltpu.CompilerParams(collective_id=0, has_side_effects=True, vmem_limit_bytes=56 << 20),
     )(master_down.reshape(1536, 512), router_weight.T, router_gain.reshape(1, 512))
-    down, scale, router = pl.pallas_call(
+    down, scale, router, gathered = pl.pallas_call(
         write_kernel,
         name="write",
         out_shape=(
             jax.ShapeDtypeStruct((1536, 2048), BF16),
             jax.ShapeDtypeStruct((2, 768), F32),
             jax.ShapeDtypeStruct((2048, 128), BF16),
+            pltpu.VMEM((3, 1536, 512), BF16),
         ),
         in_specs=[vmem] * 3,
-        out_specs=[hbm] * 3,
+        out_specs=[hbm] * 3 + [vmem],
+        input_output_aliases={0: 3},
         scratch_shapes=[dma((3,))],
         compiler_params=pltpu.CompilerParams(vmem_limit_bytes=1 << 20),
     )(gathered, scale, router)
+    far = pl.pallas_call(
+        forward_kernel,
+        name="forward",
+        out_shape=pltpu.VMEM((1536, 512), BF16),
+        in_specs=[vmem],
+        out_specs=vmem,
+        scratch_shapes=[dma(())] * 4,
+        compiler_params=pltpu.CompilerParams(collective_id=1, has_side_effects=True, vmem_limit_bytes=1 << 20),
+    )(gathered)
+    down = pl.pallas_call(
+        last_kernel,
+        name="last",
+        out_shape=jax.ShapeDtypeStruct((1536, 2048), BF16),
+        in_specs=[hbm, vmem],
+        out_specs=hbm,
+        scratch_shapes=[dma(())],
+        input_output_aliases={0: 0},
+        compiler_params=pltpu.CompilerParams(vmem_limit_bytes=48 << 20),
+    )(down, far)
     return down.reshape(2, 768, 2048), scale, router
 
 

time: 62 us -> 60 us (0.968)
  Pallas kernels: 60.8 us -> 59.2 us
    pallas_call x1 -> x3, Pallas kernels: 58 us -> 56.8 us  [the longest x1 41.5 us: body(): pl.pallas_call(gather_kernel, name='gather', out_shape=(pltpu.VMEM((3, 15...]
where the time goes in v7:
time: 60 us; the launch traced here: 59.9 us
  Pallas kernels  59.2 us (99%)
  between operations  0.65 us (1%)
    pallas_call x1, Pallas kernels, body(): pl.pallas_call(gather_kernel, name='gather', out_shape=(pltpu.VMEM((3, 15...  41.5 us
    pallas_call x1, Pallas kernels, body(): pl.pallas_call(forward_kernel, name='forward', out_shape=pltpu.VMEM((1536...  14.2 us
    pallas_call x1, Pallas kernels, body(): pl.pallas_call(write_kernel, name='write', out_shape=(jax.ShapeDtypeStruc...  2.39 us

profile of v7, /device:TPU:2, one launch (start us, length us, event | category | flops | bytes accessed | tf_op | source)
XLA Modules:
  0.0 59.9 jit_solution(6813871621487753658)
XLA Ops:
  0.6 41.5 %gather.1 = (bf16[3,1536,512]{2,1,0:T(8,128)(2,1)S(1)}, f32[2,768]{1,0:T(2,128)S(1)}, bf16[2048,128]{1,0:T(8,128)(2,1)S(1)}) custom-call(f32[1536,512]{1,0:T(8,128)} %bitcast.5, f32[2,512]{1,0:T(2,128)} %bitcast.6, f32[1,512]{1,0:T(1,128)} %bitcast.7), custom_call_target="tpu_custom_call" | custom-call | tf_op jit(solution)/shard_map/gather/pallas_call | solution.py:356
  42.1 2.4 %write.1 = (bf16[1536,2048]{1,0:T(8,128)(2,1)}, f32[2,768]{1,0:T(2,128)}, bf16[2048,128]{1,0:T(8,128)(2,1)}, bf16[3,1536,512]{2,1,0:T(8,128)(2,1)S(1)}) custom-call(bf16[3,1536,512]{2,1,0:T(8,128)(2,1)S(1)} %get-tuple-element.10.gathered, f32[2,768]{1,0:T(2,128)S(1)} %get-tuple-element.11.scale, ...), custom_call_target="tpu_custom_call", output_to_operand_aliasing={{3}: (0, {})} | custom-call | tf_op jit(solution)/shard_map/write/pallas_call | solution.py:381
  44.5 14.2 %forward.1.far = bf16[1536,512]{1,0:T(8,128)(2,1)S(1)} custom-call(bf16[3,1536,512]{2,1,0:T(8,128)(2,1)S(1)} %get-tuple-element.14.gathered), custom_call_target="tpu_custom_call" | custom-call | tf_op jit(solution)/shard_map/forward/pallas_call | solution.py:396
  58.7 1.2 %last.1 = bf16[1536,2048]{1,0:T(8,128)(2,1)} custom-call(bf16[1536,2048]{1,0:T(8,128)(2,1)} %get-tuple-element.13.down_in, bf16[1536,512]{1,0:T(8,128)(2,1)S(1)} %forward.1.far), custom_call_target="tpu_custom_call", output_to_operand_aliasing={{}: (0, {})} | custom-call | tf_op jit(solution)/shard_map/last/pallas_call | solution.py:405

commit v8 on v7

--- a/solution.py
+++ b/solution.py
@@ -13,9 +13,8 @@
 BLOCK = 128
 GROUPS = BLOCK // 8
 PARTS = ((0, 2), (2, 7), (7, 12))
-CHUNKS = ((0, 1), (1, 2), (2, 4), (4, 12))
-LEAD = 512
-HALF = 768
+CHUNKS = ((0, 1), (1, 2), (2, 7), (7, 12))
+SOON = 896
 SHIFT = 32
 RAW = 32
 
@@ -47,7 +46,7 @@
     gathered, scale_out, router_out,
     rows, raw, sums, wide, weight, gains, pieces, tall,
     load_sem, small_sem, sum_send, sum_recv, raw_send, raw_recv,
-    lead_send, rest_send, up_recv, down_recv, group_ready, other_ready, turn,
+    own_send, onward_send, up_recv, down_recv, onward_recv, group_ready, other_ready,
     row_send, row_recv, col_send, rc_recv, rx_recv, zu_recv, zd_recv,
 ):
     z, x, core, y = (lax.axis_index(a) for a in ("z", "x", "core", "shard"))
@@ -171,9 +170,9 @@
     def send_chunk(c):
         lo, hi = CHUNKS[c][0] * BLOCK, min(CHUNKS[c][1] * BLOCK, first_raw)
         here, view = gathered.at[0, pl.ds(lo, hi - lo)], pl.ds(lo, hi - lo)
-        semaphore = lead_send if hi <= LEAD else rest_send
-        send(here, gathered.at[1, view], semaphore, up_recv, at_y(1))
-        send(here, gathered.at[2, view], semaphore, down_recv, at_y(ny - 1))
+        k = 0 if hi <= SOON else 1
+        send(here, gathered.at[1, view], own_send, up_recv.at[k], at_y(1))
+        send(here, gathered.at[2, view], own_send, down_recv.at[k], at_y(ny - 1))
 
     for c in range(4):
         if c == 0:
@@ -182,9 +181,7 @@
             finish_sums(1, (1, 2))
         rescale(c)
 
-        @pl.when(core == 1)
-        def _(c=c):
-            send_chunk(c)
+        send_chunk(c)
 
     done(raw, raw_recv)
     last = column(inverse, 11)[BLOCK - RAW :]
@@ -206,17 +203,6 @@
     @pl.when(ordinary)
     def _():
         pl.semaphore_wait(other_ready, 1)
-
-    @pl.when(core == 1)
-    def _():
-        done(both(LEAD), lead_send)
-        tell(turn, [partner])
-
-    @pl.when(core == 0)
-    def _():
-        pl.semaphore_wait(turn, 1)
-        for c in range(4):
-            send_chunk(c)
 
     view = pieces.at[:, mine]
     send(view, view, col_send, rc_recv, partner)
@@ -241,6 +227,15 @@
                 done(plane(0), zd_recv.at[k - 1])
             send(plane(k), plane(k), col_send, zd_recv.at[k], at_z(nz - 1))
 
+    done(gathered.at[0, pl.ds(0, SOON)], up_recv.at[0])
+    done(gathered.at[0, pl.ds(0, SOON)], down_recv.at[0])
+
+    @pl.when(core == 0)
+    def _():
+        lower, upper = pl.ds(0, SOON // 2), pl.ds(SOON // 2, SOON // 2)
+        send(gathered.at[1, lower], gathered.at[3, lower], onward_send, onward_recv, at_y(1))
+        send(gathered.at[2, upper], gathered.at[3, upper], onward_send, onward_recv, at_y(ny - 1))
+
     done(plane(0), zu_recv.at[3])
     done(plane(0), zd_recv.at[2])
 
@@ -258,13 +253,14 @@
     done(raw, raw_send)
     done(pieces.at[pl.ds(0, ny - 1), 0], row_send)
     done(pieces.at[:, pl.ds(0, 63)], col_send)
+    done(both(first_raw), own_send)
+    done(gathered.at[0, pl.ds(0, first_raw - SOON)], up_recv.at[1])
+    done(gathered.at[0, pl.ds(0, first_raw - SOON)], down_recv.at[1])
+
     @pl.when(core == 0)
     def _():
-        done(both(LEAD), lead_send)
-
-    done(both(first_raw - LEAD), rest_send)
-    done(gathered.at[0, pl.ds(0, first_raw)], up_recv)
-    done(gathered.at[0, pl.ds(0, first_raw)], down_recv)
+        done(gathered.at[0, pl.ds(0, SOON)], onward_send)
+        done(gathered.at[0, pl.ds(0, SOON)], onward_recv)
 
 
 def write_kernel(gathered, scale, router, down_out, scale_out, router_out, same, sems):
@@ -278,6 +274,15 @@
     copies.append(pltpu.make_async_copy(router, router_out, sems.at[2]))
     for copy in copies:
         copy.start()
+
+    @pl.when(lax.axis_index("core") == 0)
+    def _():
+        columns = pl.ds(pl.multiple_of(lax.rem(y + 2, 4) * 512, 512), 512)
+        view = pl.ds(0, SOON)
+        copy = pltpu.make_async_copy(gathered.at[3, view], down_out.at[view, columns], sems.at[3])
+        copy.start()
+        copy.wait()
+
     done(down_out.at[:, pl.ds(0, 3 * 512)], sems.at[0])
     copies[3].wait()
     copies[4].wait()
@@ -302,51 +307,66 @@
             device_id_type=MESH,
         ).start()
 
-    end = 12 * BLOCK
-    send(1, 0, HALF - SHIFT, up_send, up_recv, up)
-    send(2, HALF, end, down_send, down_recv, down)
-
-    @pl.when(y < ny - 1)
-    def _():
-        send(1, HALF - SHIFT, HALF, up_send, up_recv, up)
-
-    @pl.when(y == 1)
-    def _():
-        send(2, HALF - SHIFT, HALF, down_send, down_recv, down)
-
-    @pl.when(y == ny - 1)
-    def _():
-        done(far.at[pl.ds(0, HALF - SHIFT)], up_send)
-
-    @pl.when(y < ny - 1)
-    def _():
-        done(far.at[pl.ds(0, HALF)], up_send)
-
-    @pl.when(y == 1)
-    def _():
-        done(far.at[pl.ds(0, end - HALF + SHIFT)], down_send)
-
-    @pl.when(y != 1)
-    def _():
-        done(far.at[pl.ds(0, end - HALF)], down_send)
-
-    @pl.when(y == 0)
-    def _():
-        done(far.at[pl.ds(0, HALF - SHIFT)], up_recv)
-        done(far.at[pl.ds(0, end - HALF + SHIFT)], down_recv)
-
-    @pl.when(y > 0)
-    def _():
-        done(far.at[pl.ds(0, HALF)], up_recv)
-        done(far.at[pl.ds(0, end - HALF)], down_recv)
+    def onwards(first):
+        end = 12 * BLOCK
+        half = (first + end) // 2
+        send(1, first, half - SHIFT, up_send, up_recv, up)
+        send(2, half, end, down_send, down_recv, down)
+
+        @pl.when(y < ny - 1)
+        def _():
+            send(1, half - SHIFT, half, up_send, up_recv, up)
+
+        @pl.when(y == 1)
+        def _():
+            send(2, half - SHIFT, half, down_send, down_recv, down)
+
+        @pl.when(y == ny - 1)
+        def _():
+            done(far.at[pl.ds(0, half - SHIFT - first)], up_send)
+
+        @pl.when(y < ny - 1)
+        def _():
+            done(far.at[pl.ds(0, half - first)], up_send)
+
+        @pl.when(y == 1)
+        def _():
+            done(far.at[pl.ds(0, end - half + SHIFT)], down_send)
+
+        @pl.when(y != 1)
+        def _():
+            done(far.at[pl.ds(0, end - half)], down_send)
+
+        @pl.when(y == 0)
+        def _():
+            done(far.at[pl.ds(0, half - SHIFT - first)], up_recv)
+            done(far.at[pl.ds(0, end - half + SHIFT)], down_recv)
+
+        @pl.when(y > 0)
+        def _():
+            done(far.at[pl.ds(0, half - first)], up_recv)
+            done(far.at[pl.ds(0, end - half)], down_recv)
+
+    @pl.when(core == 0)
+    def _():
+        onwards(SOON)
+
+    @pl.when(core == 1)
+    def _():
+        onwards(0)
 
 
 def last_kernel(down_in, far, down_out, sem):
     s = lax.rem(lax.axis_index("shard") + 2, 4)
     columns = pl.ds(pl.multiple_of(s * 512, 512), 512)
-    copy = pltpu.make_async_copy(far, down_out.at[:, columns], sem)
-    copy.start()
-    copy.wait()
+    for core, first in ((0, SOON), (1, 0)):
+
+        @pl.when(lax.axis_index("core") == core)
+        def _(first=first):
+            view = pl.ds(first, 12 * BLOCK - first)
+            copy = pltpu.make_async_copy(far.at[view], down_out.at[view, columns], sem)
+            copy.start()
+            copy.wait()
 
 
 def body(master_down, router_weight, router_gain):
@@ -357,7 +377,7 @@
         gather_kernel,
         name="gather",
         out_shape=(
-            pltpu.VMEM((3, 1536, 512), BF16),
+            pltpu.VMEM((4, 1536, 512), BF16),
             pltpu.VMEM((2, 768), F32),
             pltpu.VMEM((2048, 128), BF16),
         ),
@@ -373,7 +393,7 @@
             pltpu.VMEM((4, 64, 2, 512), BF16),
             pltpu.VMEM((128, 2048), F32),
             dma((3,)), dma((2,)), dma(()), dma((2,)), dma(()), dma(()),
-            dma(()), dma(()), dma(()), dma(()), regular, regular, regular,
+            dma(()), dma(()), dma((2,)), dma((2,)), dma(()), regular, regular,
             dma(()), dma(()), dma(()), dma(()), dma((2,)), dma((4,)), dma((3,)),
         ],
         compiler_params=pltpu.CompilerParams(collective_id=0, has_side_effects=True, vmem_limit_bytes=56 << 20),
@@ -385,12 +405,12 @@
             jax.ShapeDtypeStruct((1536, 2048), BF16),
             jax.ShapeDtypeStruct((2, 768), F32),
             jax.ShapeDtypeStruct((2048, 128), BF16),
-            pltpu.VMEM((3, 1536, 512), BF16),
+            pltpu.VMEM((4, 1536, 512), BF16),
         ),
         in_specs=[vmem] * 3,
         out_specs=[hbm] * 3 + [vmem],
         input_output_aliases={0: 3},
-        scratch_shapes=[dma((3,))],
+        scratch_shapes=[dma((4,))],
         compiler_params=pltpu.CompilerParams(vmem_limit_bytes=1 << 20),
     )(gathered, scale, router)
     far = pl.pallas_call(

time: 60 us -> 59.2 us (0.987)
  Pallas kernels: 59.2 us -> 58.5 us
    pallas_call x1, Pallas kernels: 14.2 us -> 8.49 us  [body(): pl.pallas_call(forward_kernel, name='forward', out_shape=pltpu.VMEM((1536...]
    pallas_call x1, Pallas kernels: 41.5 us -> 46.4 us  [body(): pl.pallas_call(gather_kernel, name='gather', out_shape=(pltpu.VMEM((4, 15...]
where the time goes in v8:
time: 59.2 us; the launch traced here: 59.1 us
  Pallas kernels  58.5 us (99%)
  between operations  0.65 us (1%)
    pallas_call x1, Pallas kernels, body(): pl.pallas_call(gather_kernel, name='gather', out_shape=(pltpu.VMEM((4, 15...  46.4 us
    pallas_call x1, Pallas kernels, body(): pl.pallas_call(forward_kernel, name='forward', out_shape=pltpu.VMEM((1536...  8.49 us
    pallas_call x1, Pallas kernels, body(): pl.pallas_call(write_kernel, name='write', out_shape=(jax.ShapeDtypeStruc...  2.69 us

profile of v8, /device:TPU:2, one launch (start us, length us, event | category | flops | bytes accessed | tf_op | source)
XLA Modules:
  0.0 59.1 jit_solution(11320621272537375447)
XLA Ops:
  0.6 46.4 %gather.1 = (bf16[4,1536,512]{2,1,0:T(8,128)(2,1)S(1)}, f32[2,768]{1,0:T(2,128)S(1)}, bf16[2048,128]{1,0:T(8,128)(2,1)S(1)}) custom-call(f32[1536,512]{1,0:T(8,128)} %bitcast.5, f32[2,512]{1,0:T(2,128)} %bitcast.6, f32[1,512]{1,0:T(1,128)} %bitcast.7), custom_call_target="tpu_custom_call" | custom-call | tf_op jit(solution)/shard_map/gather/pallas_call | solution.py:376
  47.1 2.7 %write.1 = (bf16[1536,2048]{1,0:T(8,128)(2,1)}, f32[2,768]{1,0:T(2,128)}, bf16[2048,128]{1,0:T(8,128)(2,1)}, bf16[4,1536,512]{2,1,0:T(8,128)(2,1)S(1)}) custom-call(bf16[4,1536,512]{2,1,0:T(8,128)(2,1)S(1)} %get-tuple-element.10.gathered, f32[2,768]{1,0:T(2,128)S(1)} %get-tuple-element.11.scale, ...), custom_call_target="tpu_custom_call", output_to_operand_aliasing={{3}: (0, {})} | custom-call | tf_op jit(solution)/shard_map/write/pallas_call | solution.py:401
  49.8 8.5 %forward.1.far = bf16[1536,512]{1,0:T(8,128)(2,1)S(1)} custom-call(bf16[4,1536,512]{2,1,0:T(8,128)(2,1)S(1)} %get-tuple-element.14.gathered), custom_call_target="tpu_custom_call" | custom-call | tf_op jit(solution)/shard_map/forward/pallas_call | solution.py:416
  58.3 0.9 %last.1 = bf16[1536,2048]{1,0:T(8,128)(2,1)} custom-call(bf16[1536,2048]{1,0:T(8,128)(2,1)} %get-tuple-element.13.down_in, bf16[1536,512]{1,0:T(8,128)(2,1)S(1)} %forward.1.far), custom_call_target="tpu_custom_call", output_to_operand_aliasing={{}: (0, {})} | custom-call | tf_op jit(solution)/shard_map/last/pallas_call | solution.py:425

commit v9 on v8

--- a/solution.py
+++ b/solution.py
@@ -16,7 +16,7 @@
 CHUNKS = ((0, 1), (1, 2), (2, 7), (7, 12))
 SOON = 896
 SHIFT = 32
-RAW = 32
+RAW = 48
 
 
 def part_of(block):

time: 59.2 us -> 59.2 us (level)
  no operation moved by 1% of the time
where the time goes in v9:
time: 59.2 us; the launch traced here: 59.1 us
  Pallas kernels  58.4 us (99%)
  between operations  0.65 us (1%)
    pallas_call x1, Pallas kernels, body(): pl.pallas_call(gather_kernel, name='gather', out_shape=(pltpu.VMEM((4, 15...  46.1 us
    pallas_call x1, Pallas kernels, body(): pl.pallas_call(forward_kernel, name='forward', out_shape=pltpu.VMEM((1536...  8.73 us
    pallas_call x1, Pallas kernels, body(): pl.pallas_call(write_kernel, name='write', out_shape=(jax.ShapeDtypeStruc...  2.69 us

profile of v9, /device:TPU:2, one launch (start us, length us, event | category | flops | bytes accessed | tf_op | source)
XLA Modules:
  0.0 59.1 jit_solution(14373782486574144120)
XLA Ops:
  0.6 46.1 %gather.1 = (bf16[4,1536,512]{2,1,0:T(8,128)(2,1)S(1)}, f32[2,768]{1,0:T(2,128)S(1)}, bf16[2048,128]{1,0:T(8,128)(2,1)S(1)}) custom-call(f32[1536,512]{1,0:T(8,128)} %bitcast.5, f32[2,512]{1,0:T(2,128)} %bitcast.6, f32[1,512]{1,0:T(1,128)} %bitcast.7), custom_call_target="tpu_custom_call" | custom-call | tf_op jit(solution)/shard_map/gather/pallas_call | solution.py:376
  46.8 2.7 %write.1 = (bf16[1536,2048]{1,0:T(8,128)(2,1)}, f32[2,768]{1,0:T(2,128)}, bf16[2048,128]{1,0:T(8,128)(2,1)}, bf16[4,1536,512]{2,1,0:T(8,128)(2,1)S(1)}) custom-call(bf16[4,1536,512]{2,1,0:T(8,128)(2,1)S(1)} %get-tuple-element.10.gathered, f32[2,768]{1,0:T(2,128)S(1)} %get-tuple-element.11.scale, ...), custom_call_target="tpu_custom_call", output_to_operand_aliasing={{3}: (0, {})} | custom-call | tf_op jit(solution)/shard_map/write/pallas_call | solution.py:401
  49.5 8.7 %forward.1.far = bf16[1536,512]{1,0:T(8,128)(2,1)S(1)} custom-call(bf16[4,1536,512]{2,1,0:T(8,128)(2,1)S(1)} %get-tuple-element.14.gathered), custom_call_target="tpu_custom_call" | custom-call | tf_op jit(solution)/shard_map/forward/pallas_call | solution.py:416
  58.2 0.9 %last.1 = bf16[1536,2048]{1,0:T(8,128)(2,1)} custom-call(bf16[1536,2048]{1,0:T(8,128)(2,1)} %get-tuple-element.13.down_in, bf16[1536,512]{1,0:T(8,128)(2,1)S(1)} %forward.1.far), custom_call_target="tpu_custom_call", output_to_operand_aliasing={{}: (0, {})} | custom-call | tf_op jit(solution)/shard_map/last/pallas_call | solution.py:425
